TPU v7x, 32 devices: a whole 2x2x4 slice. The times are simulated.
32 devices in a mesh: head: 4 (over y, core), seq: 8 (over z, x).
Axes of the slice: x: 2, y: 2, z: 4, core: 2. Of those that a mesh axis runs over, the one named last changes fastest.
Arguments:
- queries: bfloat16 [2, 4, 32, 128], P(None, None, ('head', 'seq')), may hold values from -16 to 16
- keys: bfloat16 [2, 4, 16384, 128], P(None, 'head', 'seq'), may hold values from -6 to 6
- values: bfloat16 [2, 4, 16384, 128], P(None, 'head', 'seq'), may hold values from -6 to 6
- indices: int32 [4, 8, 1024], P('head'), may hold values from 0 to 16383, as said below
- sizes: int32 [4, 8], P('head'), may hold values from 128 to 1024, as said below
- owners: int32 [4, 8], P('head'), may hold values from 0 to 7, as said below
Outputs:
- compact_values: bfloat16 [4, 24, 1024, 128], P('head', 'seq')
Inputs may be any that keep to these rules, and one draw needn't show every extreme that they name: `indices`: in each row of a head and fit, the 1024 positions are distinct and the first two are 0 and 1; only the first sizes[h,f] are used. `sizes`: multiples of 128; in each head one fit has 1024. `owners`: no index owns more than 3 fits of a head; in each head one index owns exactly 3.
All inputs are finite; a program needn't handle non-finite values.
Results may differ from a plain program's by a relative error of at most 0.008.
Values may be sent and summed in bfloat16 or wider, within the bound.
A program may use at most 128 MiB of HBM per device.

v0:
```python
import jax
import jax.numpy as jnp
from jax import lax
from jax.sharding import PartitionSpec as P

FITS_LAYER = 4
SLOTS = 3


RIDGE = 0.3


def merged(part, axis, combine):
    gathered = jax.tree.map(lambda a: lax.all_gather(a, axis), part)

    def take(source):
        return jax.tree.map(lambda a: lax.dynamic_index_in_dim(a, source, 0, False), gathered)

    return lax.fori_loop(
        1, lax.axis_size(axis), lambda source, state: combine(state, take(source)), take(0)
    )


def solve_fit(query_rows, target_rows, compact, size):
    scale = query_rows.shape[-1] ** (-0.5)
    width = compact.shape[0]
    scores = (
        lax.dot_general(
            query_rows, compact, (((1,), (1,)), ((), ())), preferred_element_type=jnp.float32
        )
        * scale
    )
    live = jnp.arange(width, dtype=jnp.int32) < size
    scores = jnp.where(live[None, :], scores, -jnp.inf)
    peak = jnp.max(scores, axis=1)
    expo = jnp.exp(scores - peak[:, None])
    probs = (expo / jnp.sum(expo, axis=1)[:, None]).astype(jnp.bfloat16)
    gram = lax.dot_general(
        probs, probs, (((0,), (0,)), ((), ())), preferred_element_type=jnp.float32
    )
    rhs = lax.dot_general(
        probs, target_rows, (((0,), (0,)), ((), ())), preferred_element_type=jnp.float32
    )
    ridge = RIDGE * jnp.trace(gram) / size.astype(jnp.float32)
    system = gram + jnp.diag(jnp.where(live, ridge, jnp.float32(1.0)))
    factor = jnp.linalg.cholesky(system)
    solution = jax.scipy.linalg.cho_solve((factor, True), rhs)
    return solution.astype(jnp.bfloat16)


def block_attend(query_block, key_rows, value_rows):
    scale = query_block.shape[-1] ** (-0.5)
    scores = (
        lax.dot_general(
            query_block, key_rows, (((1,), (1,)), ((), ())), preferred_element_type=jnp.float32
        )
        * scale
    )
    peak = jnp.max(scores, axis=1)
    weights = jnp.exp(scores - peak[:, None])
    total = jnp.sum(weights, axis=1)
    numer = jnp.dot(weights.astype(jnp.bfloat16), value_rows, preferred_element_type=jnp.float32)
    return (numer, total, peak)


def combine(first, second):
    numer_a, total_a, peak_a = first
    numer_b, total_b, peak_b = second
    peak = jnp.maximum(peak_a, peak_b)
    factor_a = jnp.exp(peak_a - peak)
    factor_b = jnp.exp(peak_b - peak)
    return (
        numer_a * factor_a[..., None] + numer_b * factor_b[..., None],
        total_a * factor_a + total_b * factor_b,
        peak,
    )


def on_device(queries, keys, values, indices, sizes, owners):
    regrouped = lax.all_to_all(queries, "head", split_axis=1, concat_axis=2, tiled=True)
    gathered = lax.all_gather(regrouped, "seq", axis=2, tiled=True)
    all_queries = gathered[:, 0]
    key_rows = keys[:, 0]
    value_rows = values[:, 0]
    layers, local_len, width = key_rows.shape
    row_count = all_queries.shape[1]
    block = 256 if row_count % 256 == 0 else row_count
    numer_list, total_list, peak_list = ([], [], [])
    for layer in range(layers):
        blocks = all_queries[layer].reshape(row_count // block, block, width)
        numer, total, peak = lax.map(
            lambda query_block: block_attend(query_block, key_rows[layer], value_rows[layer]),
            blocks,
        )
        numer_list.append(numer.reshape(row_count, width))
        total_list.append(total.reshape(row_count))
        peak_list.append(peak.reshape(row_count))
    numer = jnp.stack(numer_list)
    total = jnp.stack(total_list)
    peak = jnp.stack(peak_list)
    numer, total, peak = merged((numer, total, peak), "seq", combine)
    target = (numer / total[..., None]).astype(jnp.bfloat16)
    device = lax.axis_index("seq")
    groups = lax.axis_size("seq")
    flat_keys = key_rows.reshape(layers * local_len, width)
    fit_count = indices.shape[1]
    capacity = indices.shape[2]
    fit_ids = jnp.arange(fit_count, dtype=jnp.int32)

    def run_fit(fit, compact):
        layer = fit // FITS_LAYER
        query_rows = lax.dynamic_index_in_dim(all_queries, layer, 0, keepdims=False)
        target_rows = lax.dynamic_index_in_dim(target, layer, 0, keepdims=False)
        return solve_fit(query_rows, target_rows, compact, sizes[0, fit])

    owned = owners[0]
    earlier = jnp.sum(
        ((owned[:, None] == owned[None, :]) & (fit_ids[:, None] > fit_ids[None, :])).astype(
            jnp.int32
        ),
        axis=1,
    )
    empty = jnp.zeros((capacity, width), jnp.bfloat16)
    results = []
    work = -(-fit_count // groups)
    padded = jnp.pad(indices[0], ((0, work * groups - fit_count), (0, 0)))
    ids = jnp.arange(lax.axis_size("seq") * work, dtype=jnp.int32)
    offset = padded - device * local_len
    inside = (offset >= 0) & (offset < local_len)
    source = (jnp.minimum(ids, fit_count - 1) // FITS_LAYER)[:, None] * local_len + jnp.clip(
        offset, 0, local_len - 1
    )
    picked = jnp.take(flat_keys, source, axis=0)
    found = jnp.where(inside[..., None], picked, jnp.zeros((), picked.dtype))
    assigned = lax.psum_scatter(
        jnp.where((ids < fit_count)[:, None, None], found.astype(jnp.float32), 0.0).astype(
            jnp.bfloat16
        ),
        "seq",
        scatter_dimension=0,
        tiled=True,
    )
    fit = device * work + 0
    solved = [
        lax.cond(
            fit < fit_count,
            lambda: run_fit(jnp.minimum(fit, fit_count - 1), assigned[0]),
            lambda: empty,
        )
    ]
    fitted = lax.all_gather(jnp.stack(solved), "seq", axis=0, tiled=True)
    for slot in range(SLOTS):
        match = (owned == device) & (earlier == slot)
        fit = jnp.sum(jnp.where(match, fit_ids, 0))
        live = jnp.any(match)
        results.append(jnp.where(live, fitted[fit], empty))
    return jnp.stack(results)[None]


def solution(mesh):
    in_specs = (
        P(None, None, ("head", "seq"), None),
        P(None, "head", "seq", None),
        P(None, "head", "seq", None),
        P("head", None, None),
        P("head", None),
        P("head", None),
    )
    out_specs = P("head", "seq", None, None)
    return jax.shard_map(
        on_device, mesh=mesh, in_specs=in_specs, out_specs=out_specs, check_vma=False
    )
```

profile of v0, /device:TPU:0, one launch (start us, length us, event | category | flops | bytes accessed | tf_op | source)
XLA Modules:
  0.0 553.1 jit_solution(705433500807465498)
XLA Ops:
  7.8 4.3 all-to-all-start
  17.5 23.3 %gather_fusion = bf16[8192,128]{1,0:T(8,128)(2,1)S(1)} fusion(bf16[4096,128]{1,0:T(8,128)(2,1)} %bitcast.231, s32[8192]{0:T(1024)S(1)} %bitcast_clamp_fusion), kind=kCustom, calls=%fused_computation | custom fusion | bytes 4227072 | tf_op jit(solution)/shard_map/jit(_take)/gather | solution.py:133
  40.8 4.6 select_convert_fusion
  45.5 27.3 %all-gather = bf16[2,32,1,128]{3,0,2,1:T(2,128)(2,1)S(1)} all-gather(bf16[2,4,1,128]{3,0,2,1:T(2,128)(2,1)S(1)} %all-to-all-done), channel_id=2, replica_groups=mesh['head'=4,'seq'=8] {'seq'}, dimensions={1}, use_global_device_ids=true | all-gather | bytes 18432 | tf_op jit(solution)/shard_map/all_gather | solution.py:81
  75.4 30.9 %all-gather.1 = f32[16,32,128]{2,1,0:T(8,128)S(1)} all-gather(f32[2,32,128]{2,1,0:T(8,128)S(1)} %pad_maximum_fusion), channel_id=3, replica_groups=mesh['head'=4,'seq'=8] {'seq'}, dimensions={0}, use_global_device_ids=true | all-gather | bytes 294912 | tf_op jit(solution)/shard_map/all_gather | solution.py:14
  106.5 18.8 %all-gather.5 = f32[8,2,32]{2,1,0:T(2,128)S(1)} all-gather(f32[1,2,32]{2,1,0:T(2,128)S(1)} %maximum_bitcast_fusion.1), channel_id=4, replica_groups=mesh['head'=4,'seq'=8] {'seq'}, dimensions={0}, use_global_device_ids=true | all-gather | bytes 2304 | tf_op jit(solution)/shard_map/all_gather | solution.py:14
  125.4 16.3 %all-gather.6 = f32[8,2,32]{2,1,0:T(2,128)S(1)} all-gather(f32[1,2,32]{2,1,0:T(2,128)S(1)} %maximum_bitcast_fusion.2), channel_id=5, replica_groups=mesh['head'=4,'seq'=8] {'seq'}, dimensions={0}, use_global_device_ids=true | all-gather | bytes 2304 | tf_op jit(solution)/shard_map/all_gather | solution.py:14
  142.7 350.5 %conditional.1 = (bf16[1024,128]{1,0:T(8,128)(2,1)}) conditional(s32[]{:T(128)} %convert_element_type.31, () %tuple.37, (s32[]{:T(128)}, s32[1,8]{1,0:T(1,128)S(1)}, bf16[2,1,32,128]{3,0,2,1:T(2,128)(2,1)S(1)}, bf16[1,1024,128]{2,1,0:T(8,128)(2,1)}, bf16[2,32,128]{2,1,0:T(8,128)(2,1)S(1)}) %tuple.135), branch_computations={%region_9.10_spmd, %region_10.30_spmd} | conditional | flops 4732588032 | bytes 106631456 | solution.py:145
  145.5 3.3 select_reduce_fusion
  148.8 5.8 %copy.18 = f32[1024,1024]{0,1:T(8,128)} copy(f32[1024,1024]{1,0:T(8,128)} %get-tuple-element.347) | data formatting | bytes 8388608 | tf_op jit(solution)/shard_map/cond/branch_1_fun/dot_general | solution.py:38
  156.6 4.5 fusion.4
  161.1 1.9 copy-done.2
  163.1 11.7 %cholesky.5 = f32[128,128]{1,0:T(8,128)S(1)} custom-call(f32[128,128]{1,0:T(8,128)S(1)} %cholesky.221), custom_call_target="Cholesky" | custom-call | tf_op jit(solution)/shard_map/cond/branch_1_fun/jit(cholesky)/cholesky | solution.py:46
  174.8 2.5 cholesky.37
  177.3 9.8 %custom-call.58 = f32[1,128,128]{1,2,0:T(8,128)S(1)} custom-call(f32[1,128,128]{2,1,0:T(8,128)S(1)} %get-tuple-element.343), custom_call_target="InvertDiagBlocksLowerTriangular" | custom-call | tf_op jit(solution)/shard_map/cond/branch_1_fun/jit(cholesky)/cholesky | solution.py:46
  187.1 2.4 constant_dynamic-update-slice_fusion.48
  191.1 11.9 %cholesky.27 = f32[128,128]{1,0:T(8,128)S(1)} custom-call(f32[128,128]{1,0:T(8,128)S(1)} %cholesky.227), custom_call_target="Cholesky" | custom-call | tf_op jit(solution)/shard_map/cond/branch_1_fun/jit(cholesky)/cholesky | solution.py:46
  205.4 9.8 %custom-call.59 = f32[1,128,128]{1,2,0:T(8,128)S(1)} custom-call(f32[1,128,128]{2,1,0:T(8,128)S(1)} %get-tuple-element.340), custom_call_target="InvertDiagBlocksLowerTriangular" | custom-call | tf_op jit(solution)/shard_map/cond/branch_1_fun/jit(cholesky)/cholesky | solution.py:46
  216.5 2.1 convolution_subtract_fusion.1
  218.6 11.7 %cholesky.58 = f32[128,128]{1,0:T(8,128)S(1)} custom-call(f32[128,128]{1,0:T(8,128)S(1)} %cholesky.232), custom_call_target="Cholesky" | custom-call | tf_op jit(solution)/shard_map/cond/branch_1_fun/jit(cholesky)/cholesky | solution.py:46
  232.2 9.8 %custom-call.60 = f32[1,128,128]{1,2,0:T(8,128)S(1)} custom-call(f32[1,128,128]{2,1,0:T(8,128)S(1)} %get-tuple-element.337), custom_call_target="InvertDiagBlocksLowerTriangular" | custom-call | tf_op jit(solution)/shard_map/cond/branch_1_fun/jit(cholesky)/cholesky | solution.py:46
  243.2 2.3 convolution_subtract_fusion.2
  245.6 11.9 %cholesky.87 = f32[128,128]{1,0:T(8,128)S(1)} custom-call(f32[128,128]{1,0:T(8,128)S(1)} %cholesky.237), custom_call_target="Cholesky" | custom-call | tf_op jit(solution)/shard_map/cond/branch_1_fun/jit(cholesky)/cholesky | solution.py:46
  259.4 9.8 %custom-call.61 = f32[1,128,128]{1,2,0:T(8,128)S(1)} custom-call(f32[1,128,128]{2,1,0:T(8,128)S(1)} %get-tuple-element.334), custom_call_target="InvertDiagBlocksLowerTriangular" | custom-call | tf_op jit(solution)/shard_map/cond/branch_1_fun/jit(cholesky)/cholesky | solution.py:46
  270.3 2.3 convolution_subtract_fusion.3
  272.7 11.7 %cholesky.116 = f32[128,128]{1,0:T(8,128)S(1)} custom-call(f32[128,128]{1,0:T(8,128)S(1)} %cholesky.242), custom_call_target="Cholesky" | custom-call | tf_op jit(solution)/shard_map/cond/branch_1_fun/jit(cholesky)/cholesky | solution.py:46
  286.3 10.2 %custom-call.62 = f32[1,128,128]{1,2,0:T(8,128)S(1)} custom-call(f32[1,128,128]{2,1,0:T(8,128)S(1)} %get-tuple-element.331), custom_call_target="InvertDiagBlocksLowerTriangular" | custom-call | tf_op jit(solution)/shard_map/cond/branch_1_fun/jit(cholesky)/cholesky | solution.py:46
  297.6 2.3 convolution_subtract_fusion.4
  299.9 11.7 %cholesky.146 = f32[128,128]{1,0:T(8,128)S(1)} custom-call(f32[128,128]{1,0:T(8,128)S(1)} %cholesky.249), custom_call_target="Cholesky" | custom-call | tf_op jit(solution)/shard_map/cond/branch_1_fun/jit(cholesky)/cholesky | solution.py:46
  313.5 9.8 %custom-call.63 = f32[1,128,128]{1,2,0:T(8,128)S(1)} custom-call(f32[1,128,128]{2,1,0:T(8,128)S(1)} %get-tuple-element.328), custom_call_target="InvertDiagBlocksLowerTriangular" | custom-call | tf_op jit(solution)/shard_map/cond/branch_1_fun/jit(cholesky)/cholesky | solution.py:46
  324.3 2.0 convolution_subtract_fusion.5
  326.3 11.8 %cholesky.176 = f32[128,128]{1,0:T(8,128)S(1)} custom-call(f32[128,128]{1,0:T(8,128)S(1)} %cholesky.256), custom_call_target="Cholesky" | custom-call | tf_op jit(solution)/shard_map/cond/branch_1_fun/jit(cholesky)/cholesky | solution.py:46
  340.1 9.8 %custom-call.64 = f32[1,128,128]{1,2,0:T(8,128)S(1)} custom-call(f32[1,128,128]{2,1,0:T(8,128)S(1)} %get-tuple-element.325), custom_call_target="InvertDiagBlocksLowerTriangular" | custom-call | tf_op jit(solution)/shard_map/cond/branch_1_fun/jit(cholesky)/cholesky | solution.py:46
  350.7 1.8 convolution_subtract_fusion.16
  352.5 11.7 %cholesky.204 = f32[128,128]{1,0:T(8,128)S(1)} custom-call(f32[128,128]{1,0:T(8,128)S(1)} %convolution_subtract_fusion.16), custom_call_target="Cholesky" | custom-call | tf_op jit(solution)/shard_map/cond/branch_1_fun/jit(cholesky)/cholesky | solution.py:46
  366.3 4.8 select_select_fusion
  371.1 22.8 %while.13 = (s32[]{:T(128)}, f32[1024,1024]{1,0:T(8,128)}, s32[8,2]{0,1:T(2,128)S(1)}, f32[8,128,128]{2,1,0:T(8,128)S(1)}, s32[]{:T(128)}) while((s32[]{:T(128)}, f32[1024,1024]{1,0:T(8,128)}, s32[8,2]{0,1:T(2,128)S(1)}, f32[8,128,128]{2,1,0:T(8,128)S(1)}, s32[]{:T(128)}) %tuple.121), condition=%wide.while_cond, body=%wide.while_body.sunk | while | flops 2 | bytes 131181 | solution.py:47
  371.7 2.2 bitcast_dynamic-update-slice_fusion.2
  374.6 2.2 bitcast_dynamic-update-slice_fusion.2
  377.5 2.2 bitcast_dynamic-update-slice_fusion.2
  380.3 2.2 bitcast_dynamic-update-slice_fusion.2
  383.2 2.2 bitcast_dynamic-update-slice_fusion.2
  386.0 2.2 bitcast_dynamic-update-slice_fusion.2
  388.9 2.2 bitcast_dynamic-update-slice_fusion.2
  391.8 2.2 bitcast_dynamic-update-slice_fusion.2
  393.9 78.8 %custom-call.65 = f32[8,128,128]{1,2,0:T(8,128)S(1)} custom-call(f32[8,128,128]{2,1,0:T(8,128)S(1)} %get-tuple-element.254), custom_call_target="InvertDiagBlocksLowerTriangular" | custom-call | tf_op jit(solution)/shard_map/cond/branch_1_fun/jit(_cho_solve)/triangular_solve | solution.py:47
  499.1 43.0 %all-gather.9.cloned.1.call-done = bf16[8192,128]{1,0:T(8,128)(2,1)} async-done(((bf16[1024,128]{1,0:T(8,128)(2,1)}), bf16[8192,128]{1,0:T(8,128)(2,1)}) %all-gather.9.cloned.1.call-update) | async-done | bytes 2097168 | tf_op jit(solution)/shard_map/all_gather | solution.py:151
  542.1 3.0 dynamic-slice_select_fusion.2
  (161 shorter events, 58.1 us)
Async XLA Ops:
  7.8 37.7 %all-to-all-start = ((bf16[2,4,1,128]{3,0,2,1:T(2,128)(2,1)}), bf16[2,4,1,128]{3,0,2,1:T(2,128)(2,1)S(1)}, u32[]{:S(2)}, u32[]{:S(2)}) async-start(bf16[2,4,1,128]{3,0,2,1:T(2,128)(2,1)} %copy.19), calls=%async_computation | async-start | bytes 4096 | tf_op jit(solution)/shard_map/all_to_all | solution.py:80
  12.1 130.7 %reduce-scatter.2.cloned.1.call-start = ((), (), s32[]{:S(2)}) async-start(), calls=%async_computation.2 | async-start | bytes 2359296 | tf_op jit(solution)/shard_map/reduce_scatter | solution.py:135
  40.8 32.0 %copy-start = (bf16[2,1,2048,128]{3,2,1,0:T(8,128)(2,1)S(1)}, bf16[2,1,2048,128]{3,2,1,0:T(8,128)(2,1)}, u32[]{:S(2)}) copy-start(bf16[2,1,2048,128]{3,2,1,0:T(8,128)(2,1)} %param.11) | copy-start | bytes 3145732
  45.4 29.7 %copy-start.3 = (bf16[2,1,2048,128]{3,2,1,0:T(8,128)(2,1)S(1)}, bf16[2,1,2048,128]{3,2,1,0:T(8,128)(2,1)}, u32[]{:S(2)}) copy-start(bf16[2,1,2048,128]{3,2,1,0:T(8,128)(2,1)} %param.12) | copy-start | bytes 3145732
  45.4 97.3 %copy-start.4 = (s32[1,8]{1,0:T(1,128)S(1)}, s32[1,8]{1,0:T(1,128)}, u32[]{:S(2)}) copy-start(s32[1,8]{1,0:T(1,128)} %param.14) | copy-start | bytes 100
  45.4 496.6 %all-gather.9.cloned.1.call-start = ((), (), s32[]{:S(2)}) async-start(), calls=%async_computation.3 | async-start | bytes 2359296 | tf_op jit(solution)/shard_map/all_gather | solution.py:151
  161.1 1.9 copy-start.2
  472.8 7.0 %copy-start.1 = (f32[1024,1024]{1,0:T(8,128)S(1)}, f32[1024,1024]{1,0:T(8,128)}, u32[]{:S(2)}) copy-start(f32[1024,1024]{1,0:T(8,128)} %get-tuple-element.506) | copy-start | bytes 12582916 | tf_op jit(solution)/shard_map/cond
Sparse Core Ops, SparseCore 0:
  45.5 72.0 reduce-scatter.1
  493.4 48.5 all-gather.8
where the time goes:
time: 558 us; the launch traced here: 553 us
  other arithmetic  281 us (50%)
  blocking collectives  93.3 us (17%)
  local copies, waits for them, and re-layouts  58.9 us (11%)
  matrix products  45.8 us (8%)
  waiting for transfers between devices  43 us (8%)
  between operations  19.6 us (4%)
  loops' own time  7.19 us (1%)
    another operation x30, other arithmetic, solve_fit(): factor = jnp.linalg.cholesky(system)  172 us
    another operation x4, other arithmetic, solve_fit(): solution = jax.scipy.linalg.cho_solve((factor, True), rhs)  84.2 us
    all_gather x3, blocking collectives, merged(): gathered = jax.tree.map(lambda a: lax.all_gather(a, axis), part)  66 us
    all_gather x1, waiting for transfers between devices, on_device(): fitted = lax.all_gather(jnp.stack(solved), 'seq', axis=0, tiled=True)  43 us
    all_gather x1, blocking collectives, on_device(): gathered = lax.all_gather(regrouped, 'seq', axis=2, tiled=True)  27.3 us
    gather x1, local copies, waits for them, and re-layouts, on_device(): picked = jnp.take(flat_keys, source, axis=0)  23.3 us
    another operation x14, matrix products, solve_fit(): factor = jnp.linalg.cholesky(system)  23.1 us
    another operation x25, local copies, waits for them, and re-layouts  22.7 us
  transfers between devices with their start and end apart: 3, of which 1 were waited for; matrix products, arithmetic and copies ran while one was open for 7% of the time, Pallas kernels for 0%

commit v1 on v0

v1 whole, which is shorter than its diff:
```python
import functools

import jax
import jax.numpy as jnp
from jax import lax
from jax.experimental import pallas as pl
from jax.experimental.pallas import tpu as pltpu
from jax.sharding import PartitionSpec as P

FITS_LAYER = 4
SLOTS = 3
RIDGE = 0.3
LANES = 128
FAR = -1e30

NT = (((1,), (1,)), ((), ()))
TN = (((0,), (0,)), ((), ()))


def attend_kernel(sizes_ref, q_ref, k_ref, v_ref, idx_ref, e_ref, aux_ref, s_ref, g_ref):
    layers, rows, width = q_ref.shape
    local_len = k_ref.shape[1]
    fits, capacity = idx_ref.shape
    start = lax.axis_index("seq") * local_len
    lane = lax.broadcasted_iota(jnp.int32, (rows, LANES), 1)
    scale = width ** (-0.5)
    for layer in range(layers):
        scores = (
            lax.dot_general(q_ref[layer], k_ref[layer], NT, preferred_element_type=jnp.float32)
            * scale
        )
        s_ref[layer] = scores
        peak = jnp.max(scores, axis=1, keepdims=True)
        weights = jnp.exp(scores - peak)
        total = jnp.sum(weights, axis=1, keepdims=True)
        numer = jnp.dot(
            weights.astype(jnp.bfloat16), v_ref[layer], preferred_element_type=jnp.float32
        )
        side = jnp.where(lane < 32, total, peak)
        for fit in range(layer * FITS_LAYER, (layer + 1) * FITS_LAYER):
            aux_ref[fit, 0] = numer
            aux_ref[fit, 1] = side

    def one_fit(fit, carry):
        layer = fit // FITS_LAYER
        size = sizes_ref[0, fit]

        def one_tile(tile, top):
            base = pl.multiple_of(tile * LANES, LANES)
            drawn = idx_ref[:, pl.ds(base, LANES)]
            mine = lax.broadcasted_iota(jnp.int32, (fits, LANES), 0) == fit
            offset = jnp.sum(jnp.where(mine, drawn, 0), axis=0, keepdims=True) - start
            column = base + lax.broadcasted_iota(jnp.int32, (1, LANES), 1)
            inside = (offset >= 0) & (offset < local_len) & (column < size)
            offset = jnp.broadcast_to(jnp.where(inside, offset, -1), (rows, LANES))
            high = offset >> 7
            low = offset & (LANES - 1)
            picked = jnp.full((rows, LANES), FAR, jnp.float32)
            for block in range(local_len // LANES):
                part = s_ref[layer, :, block * LANES : (block + 1) * LANES]
                found = jnp.take_along_axis(part, low, axis=1, mode="promise_in_bounds")
                picked = jnp.where(high == block, found, picked)
            g_ref[:, pl.ds(base, LANES)] = picked
            return jnp.maximum(top, jnp.max(picked, axis=1, keepdims=True))

        top = lax.fori_loop(
            0, capacity // LANES, one_tile, jnp.full((rows, 1), FAR, jnp.float32)
        )
        picked = g_ref[...]
        expo = jnp.where(picked > 0.5 * FAR, jnp.exp(picked - top), 0.0)
        e_ref[fit] = expo.astype(jnp.bfloat16)
        aux_ref[fit, 1] = jnp.where(lane < 64, aux_ref[fit, 1], top)
        return carry

    lax.fori_loop(0, fits, one_fit, 0)


def solve_rows(system, target):
    rows = system.shape[0]
    row = lax.broadcasted_iota(jnp.int32, (rows, 1), 0)
    if rows <= 64:
        for k in range(rows):
            inverse = 1.0 / system[k : k + 1, k : k + 1]
            pivot_s = system[k : k + 1, :] * inverse
            pivot_t = target[k : k + 1, :] * inverse
            column = jnp.where(row == k, system[:, k : k + 1] - 1.0, system[:, k : k + 1])
            system = system - column * pivot_s
            target = target - column * pivot_t
        return target
    lane = lax.broadcasted_iota(jnp.int32, (1, rows), 1)

    def step(k, state):
        system, target = state
        column = jnp.sum(jnp.where(lane == k, system, 0.0), axis=1, keepdims=True)
        here = row == k
        inverse = 1.0 / jnp.sum(jnp.where(here, column, 0.0), axis=0, keepdims=True)
        pivot_s = jnp.sum(jnp.where(here, system, 0.0), axis=0, keepdims=True) * inverse
        pivot_t = jnp.sum(jnp.where(here, target, 0.0), axis=0, keepdims=True) * inverse
        column = jnp.where(here, column - 1.0, column)
        return system - column * pivot_s, target - column * pivot_t

    return lax.fori_loop(0, rows, step, (system, target))[1]


def merge_fit(e_at, aux_at, groups, size):
    first = aux_at(0, 1)
    peak, top = first[:, 32:33], first[:, 64:65]
    for source in range(1, groups):
        side = aux_at(source, 1)
        peak = jnp.maximum(peak, side[:, 32:33])
        top = jnp.maximum(top, side[:, 64:65])
    numer, total, probs = 0.0, 0.0, 0.0
    for source in range(groups):
        side = aux_at(source, 1)
        factor = jnp.exp(side[:, 32:33] - peak)
        numer = numer + aux_at(source, 0) * factor
        total = total + side[:, 0:1] * factor
        probs = probs + e_at(source).astype(jnp.float32) * jnp.exp(side[:, 64:65] - top)
    target = (numer / total).astype(jnp.bfloat16).astype(jnp.float32)
    probs = probs / jnp.sum(probs, axis=1, keepdims=True)
    return probs.astype(jnp.bfloat16), target


def fit_rows(probs, target, size):
    rows = probs.shape[0]
    gram = lax.dot_general(probs, probs, NT, preferred_element_type=jnp.float32)
    diagonal = lax.broadcasted_iota(jnp.int32, (rows, rows), 0) == lax.broadcasted_iota(
        jnp.int32, (rows, rows), 1
    )
    trace = jnp.sum(jnp.where(diagonal, gram, 0.0))
    ridge = RIDGE * trace / size
    return solve_rows(jnp.where(diagonal, gram + ridge, gram), target)


def solve_kernel(sizes_ref, e_ref, aux_ref, p_ref, x_ref):
    groups = e_ref.shape[0]
    fits = sizes_ref.shape[1]
    fit = jnp.minimum(lax.axis_index("seq"), fits - 1)
    size = sizes_ref[0, fit].astype(jnp.float32)
    probs, target = merge_fit(
        lambda s: e_ref[s], lambda s, part: aux_ref[s, part], groups, size
    )
    p_ref[...] = probs
    x_ref[...] = fit_rows(probs, target, size)


def place_kernel(slot_ref, p_ref, x_ref, out_ref):
    for slot in range(SLOTS):
        fit = slot_ref[0, slot]
        live = slot_ref[1, slot]

        @pl.when(live > 0)
        def _():
            probs = p_ref[fit]
            rows = x_ref[fit]
            high = rows.astype(jnp.bfloat16)
            low = (rows - high.astype(jnp.float32)).astype(jnp.bfloat16)
            out_ref[0, slot] = lax.dot_general(
                jnp.concatenate([probs, probs], axis=0),
                jnp.concatenate([high, low], axis=0),
                TN,
                preferred_element_type=jnp.float32,
            ).astype(jnp.bfloat16)

        @pl.when(live == 0)
        def _():
            out_ref[0, slot] = jnp.zeros(out_ref.shape[2:], jnp.bfloat16)


VMEM = pl.BlockSpec(memory_space=pltpu.VMEM)
SMEM = pl.BlockSpec(memory_space=pltpu.SMEM)
PARAMS = dict(vmem_limit_bytes=60 * 1024 * 1024)


def on_device(queries, keys, values, indices, sizes, owners):
    regrouped = lax.all_to_all(queries, "head", split_axis=1, concat_axis=2, tiled=True)
    gathered = lax.all_gather(regrouped, "seq", axis=2, tiled=True)
    all_queries = gathered[:, 0]
    layers, rows, width = all_queries.shape
    key_rows = keys[:, 0]
    value_rows = values[:, 0]
    local_len = key_rows.shape[1]
    fits, capacity = indices.shape[1:]
    groups = lax.axis_size("seq")
    expo, aux = pl.pallas_call(
        attend_kernel,
        out_shape=(
            jax.ShapeDtypeStruct((fits, rows, capacity), jnp.bfloat16),
            jax.ShapeDtypeStruct((fits, 2, rows, width), jnp.float32),
        ),
        in_specs=[SMEM] + [VMEM] * 4,
        out_specs=(VMEM, VMEM),
        scratch_shapes=[
            pltpu.VMEM((layers, rows, local_len), jnp.float32),
            pltpu.VMEM((rows, capacity), jnp.float32),
        ],
        compiler_params=pltpu.CompilerParams(**PARAMS),
    )(sizes, all_queries, key_rows, value_rows, indices[0])
    if groups > fits:
        spare = groups - fits
        expo = jnp.pad(expo, ((0, spare), (0, 0), (0, 0)))
        aux = jnp.pad(aux, ((0, spare), (0, 0), (0, 0), (0, 0)))
    expo = lax.all_to_all(expo, "seq", split_axis=0, concat_axis=0, tiled=True)
    aux = lax.all_to_all(aux, "seq", split_axis=0, concat_axis=0, tiled=True)
    probs, solved = pl.pallas_call(
        solve_kernel,
        out_shape=(
            jax.ShapeDtypeStruct((rows, capacity), jnp.bfloat16),
            jax.ShapeDtypeStruct((rows, width), jnp.float32),
        ),
        in_specs=[SMEM] + [VMEM] * 2,
        out_specs=(VMEM, VMEM),
        compiler_params=pltpu.CompilerParams(**PARAMS),
    )(sizes, expo, aux)
    probs = lax.all_gather(probs, "seq")[:fits]
    solved = lax.all_gather(solved, "seq")[:fits]
    return place(owners, probs, solved, capacity)


def place(owners, probs, solved, capacity):
    width = solved.shape[-1]
    owned = owners[0]
    fits = owned.shape[0]
    fit_ids = jnp.arange(fits, dtype=jnp.int32)
    same = owned[:, None] == owned[None, :]
    earlier = jnp.sum((same & (fit_ids[:, None] > fit_ids[None, :])).astype(jnp.int32), axis=1)
    match = (owned == lax.axis_index("seq"))[None, :] & (
        earlier[None, :] == jnp.arange(SLOTS, dtype=jnp.int32)[:, None]
    )
    chosen = jnp.sum(jnp.where(match, fit_ids[None, :], 0), axis=1)
    live = jnp.any(match, axis=1).astype(jnp.int32)
    return pl.pallas_call(
        place_kernel,
        out_shape=jax.ShapeDtypeStruct((1, SLOTS, capacity, width), jnp.bfloat16),
        in_specs=[SMEM, VMEM, VMEM],
        out_specs=VMEM,
        compiler_params=pltpu.CompilerParams(**PARAMS),
    )(jnp.stack([chosen, live]), probs, solved)


def solution(mesh):
    in_specs = (
        P(None, None, ("head", "seq"), None),
        P(None, "head", "seq", None),
        P(None, "head", "seq", None),
        P("head", None, None),
        P("head", None),
        P("head", None),
    )
    out_specs = P("head", "seq", None, None)
    return jax.shard_map(
        on_device, mesh=mesh, in_specs=in_specs, out_specs=out_specs, check_vma=False
    )
```

time: 558 us -> 155 us (0.28)
  other arithmetic: 281 us -> 0.97 us
  local copies, waits for them, and re-layouts: 58.9 us -> 2.73 us
  matrix products: 45.8 us -> 0 us
  waiting for transfers between devices: 43 us -> 8.56 us
  Pallas kernels: 0 us -> 25.6 us
  blocking collectives: 93.3 us -> 113 us
  between operations: 19.6 us -> 0.04 us
  loops' own time: 7.19 us -> 0 us
    another operation x35 -> x1, other arithmetic: 257 us -> 0.55 us  [place(): jnp.stack([chosen, live])]
    all_gather x1 -> x0, waiting for transfers between devices: 43 us -> none  [on_device(): fitted = lax.all_gather(jnp.stack(solved), 'seq', axis=0, tiled=True)]
    another operation x44 -> x0, matrix products: 38.5 us -> none  [the longest x14 23.1 us: solve_fit(): factor = jnp.linalg.cholesky(system)]
    pallas_call x0 -> x3, Pallas kernels: none -> 25.6 us  [the longest x1 18.4 us: on_device(): pl.pallas_call(attend_kernel, out_shape=(jax.ShapeDtypeStruct((fits, rows...]
    another operation x37 -> x0, local copies, waits for them, and re-layouts: 25.3 us -> none
    gather x1 -> x0, local copies, waits for them, and re-layouts: 23.3 us -> none  [on_device(): picked = jnp.take(flat_keys, source, axis=0)]
    all_to_all x0 -> x2, blocking collectives: none -> 20.1 us  [the longest x1 12.3 us: on_device(): aux = lax.all_to_all(aux, 'seq', split_axis=0, concat_axis=0, tiled=True)]
    all_to_all x1, waiting for transfers between devices: 0.01 us -> 8.56 us  [on_device(): expo = lax.all_to_all(expo, 'seq', split_axis=0, concat_axis=0, tiled=True)]
  transfers between devices with their start and end apart: 3 -> 1, of which waited for: 1 -> 1; matrix products, arithmetic and copies ran while one was open for 7% -> 1% of each run, Pallas kernels for 0% -> 0%
where the time goes in v1:
time: 155 us; the launch traced here: 154 us
  blocking collectives  113 us (73%)
  Pallas kernels  25.6 us (17%)
  waiting for transfers between devices  8.56 us (6%)
  starting transfers between devices  3.49 us (2%)
  local copies, waits for them, and re-layouts  2.73 us (2%)
    all_gather x1, blocking collectives, on_device(): probs = lax.all_gather(probs, 'seq')[:fits]  33.4 us
    all_gather x1, blocking collectives, on_device(): solved = lax.all_gather(solved, 'seq')[:fits]  32.9 us
    all_gather x1, blocking collectives, on_device(): gathered = lax.all_gather(regrouped, 'seq', axis=2, tiled=True)  26.4 us
    pallas_call x1, Pallas kernels, on_device(): pl.pallas_call(attend_kernel, out_shape=(jax.ShapeDtypeStruct((fits, rows...  18.4 us
    all_to_all x1, blocking collectives, on_device(): aux = lax.all_to_all(aux, 'seq', split_axis=0, concat_axis=0, tiled=True)  12.3 us
    all_to_all x1, waiting for transfers between devices, on_device(): expo = lax.all_to_all(expo, 'seq', split_axis=0, concat_axis=0, tiled=True)  8.56 us
    all_to_all x1, blocking collectives, on_device(): lax.all_to_all(queries, 'head', split_axis=1, concat_axis=2, tiled=True)  7.83 us
    pallas_call x1, Pallas kernels, on_device(): pl.pallas_call(solve_kernel, out_shape=(jax.ShapeDtypeStruct((rows, capac...  4.9 us
  transfers between devices with their start and end apart: 1, of which 1 were waited for; matrix products, arithmetic and copies ran while one was open for 1% of the time, Pallas kernels for 0%

profile of v1, /device:TPU:0, one launch (start us, length us, event | category | flops | bytes accessed | tf_op | source)
XLA Modules:
  0.0 154.3 jit_solution(2896042174908926330)
XLA Ops:
  0.0 0.7 copy.10
  0.7 7.8 %all_to_all.22 = bf16[2,4,1,128]{3,0,2,1:T(2,128)(2,1)S(1)} all-to-all(bf16[2,4,1,128]{3,0,2,1:T(2,128)(2,1)S(1)} %copy.10), channel_id=1, replica_groups=mesh['head'=4,'seq'=8] {'head'}, dimensions={1} | all-to-all | bytes 4096 | tf_op jit(solution)/shard_map/all_to_all | solution.py:176
  8.5 26.4 %all-gather = bf16[2,32,1,128]{3,0,2,1:T(2,128)(2,1)S(1)} all-gather(bf16[2,4,1,128]{3,0,2,1:T(2,128)(2,1)S(1)} %all_to_all.22), channel_id=2, replica_groups=mesh['head'=4,'seq'=8] {'seq'}, dimensions={1}, use_global_device_ids=true | all-gather | bytes 18432 | tf_op jit(solution)/shard_map/all_gather | solution.py:177
  35.0 0.6 copy.13
  35.6 18.4 %shard_map.64 = (bf16[8,32,1024]{2,1,0:T(8,128)(2,1)}, f32[8,2,32,128]{3,2,1,0:T(8,128)}) custom-call(s32[1,8]{1,0:T(1,128)} %sizes_ref.3, bf16[2,32,128]{2,1,0:T(8,128)(2,1)} %bitcast.18, bf16[2,2048,128]{2,1,0:T(8,128)(2,1)} %bitcast.15, bf16[2,2048,128]{2,1,0:T(8,128)(2,1)} %bitcast.16, s32[8,1024]{1,0:T(8,128)} %bitcast.19), custom_call_target="tpu_custom_call" | custom-call | tf_op jit(solution)/shard_map/pallas_call | solution.py:185
  53.9 12.3 %all_to_all.23.aux_ref = f32[8,2,32,128]{3,2,1,0:T(8,128)} all-to-all(f32[8,2,32,128]{3,2,1,0:T(8,128)} %get-tuple-element.10), channel_id=1, replica_groups=mesh['head'=4,'seq'=8] {'seq'}, dimensions={0} | all-to-all | bytes 524288 | tf_op jit(solution)/shard_map/all_to_all | solution.py:204
  66.2 3.5 %all-to-all-start.1 = ((bf16[8,32,1024]{2,1,0:T(8,128)(2,1)}), bf16[8,32,1024]{2,1,0:T(8,128)(2,1)S(1)}, u32[]{:S(2)}, u32[]{:S(2)}) async-start(bf16[8,32,1024]{2,1,0:T(8,128)(2,1)} %get-tuple-element.9), calls=%async_computation.1 | async-start | bytes 1048576 | tf_op jit(solution)/shard_map/all_to_all | solution.py:203
  69.7 0.0 copy-start.2
  69.7 0.6 copy-done.2
  70.4 0.2 convert_reduce_fusion
  70.6 0.1 fusion.2
  70.7 0.1 select_reduce_fusion
  70.8 0.5 pad_add_fusion.slot_ref
  71.4 8.6 %all-to-all-done.1.e_ref = bf16[8,32,1024]{2,1,0:T(8,128)(2,1)S(1)} async-done(((bf16[8,32,1024]{2,1,0:T(8,128)(2,1)}), bf16[8,32,1024]{2,1,0:T(8,128)(2,1)S(1)}, u32[]{:S(2)}, u32[]{:S(2)}) %all-to-all-start.1) | async-done | bytes 524320 | tf_op jit(solution)/shard_map/all_to_all | solution.py:203
  79.9 0.0 copy-start
  79.9 0.8 copy-done
  80.7 4.9 %shard_map.65 = (bf16[32,1024]{1,0:T(8,128)(2,1)}, f32[32,128]{1,0:T(8,128)}) custom-call(s32[1,8]{1,0:T(1,128)} %sizes_ref.3, bf16[8,32,1024]{2,1,0:T(8,128)(2,1)} %copy-done, f32[8,2,32,128]{3,2,1,0:T(8,128)} %all_to_all.23.aux_ref), custom_call_target="tpu_custom_call" | custom-call | tf_op jit(solution)/shard_map/pallas_call | solution.py:205
  85.6 0.0 copy-start.1
  85.6 32.9 %all-gather.2 = f32[256,128]{1,0:T(8,128)} all-gather(f32[32,128]{1,0:T(8,128)} %get-tuple-element.12), channel_id=4, replica_groups=mesh['head'=4,'seq'=8] {'seq'}, dimensions={0}, use_global_device_ids=true | all-gather | bytes 147456 | tf_op jit(solution)/shard_map/all_gather | solution.py:216
  118.6 0.0 copy-done.1
  118.6 33.4 %all-gather.1 = bf16[256,1024]{1,0:T(8,128)(2,1)} all-gather(bf16[32,1024]{1,0:T(8,128)(2,1)S(1)} %copy-done.1), channel_id=3, replica_groups=mesh['head'=4,'seq'=8] {'seq'}, dimensions={0}, use_global_device_ids=true | all-gather | bytes 589824 | tf_op jit(solution)/shard_map/all_gather | solution.py:215
  152.0 2.3 %shard_map.66 = bf16[1,3,1024,128]{3,2,1,0:T(8,128)(2,1)} custom-call(s32[2,3]{1,0:T(2,128)} %pad_add_fusion.slot_ref, bf16[8,32,1024]{2,1,0:T(8,128)(2,1)} %bitcast.14, f32[8,32,128]{2,1,0:T(8,128)} %bitcast.17), custom_call_target="tpu_custom_call" | custom-call | tf_op jit(solution)/shard_map/pallas_call | solution.py:232
  (2 shorter events, 0.0 us)
Async XLA Ops:
  66.2 13.7 %all-to-all-start.1 = ((bf16[8,32,1024]{2,1,0:T(8,128)(2,1)}), bf16[8,32,1024]{2,1,0:T(8,128)(2,1)S(1)}, u32[]{:S(2)}, u32[]{:S(2)}) async-start(bf16[8,32,1024]{2,1,0:T(8,128)(2,1)} %get-tuple-element.9), calls=%async_computation.1 | async-start | bytes 1048576 | tf_op jit(solution)/shard_map/all_to_all | solution.py:203
  69.7 0.7 copy-start.2
  79.9 0.8 copy-start
  85.6 32.9 %copy-start.1 = (bf16[32,1024]{1,0:T(8,128)(2,1)S(1)}, bf16[32,1024]{1,0:T(8,128)(2,1)}, u32[]{:S(2)}) copy-start(bf16[32,1024]{1,0:T(8,128)(2,1)} %get-tuple-element.11) | copy-start | bytes 196612

commit v2 on v1

--- a/solution.py
+++ b/solution.py
@@ -1,5 +1,3 @@
-import functools
-
 import jax
 import jax.numpy as jnp
 from jax import lax
@@ -13,20 +11,23 @@
 LANES = 128
 FAR = -1e30
 
+SUBLANES = 8
+MESH = pl.DeviceIdType.MESH
 NT = (((1,), (1,)), ((), ()))
 TN = (((0,), (0,)), ((), ()))
 
 
 def attend_kernel(sizes_ref, q_ref, k_ref, v_ref, idx_ref, e_ref, aux_ref, s_ref, g_ref):
-    layers, rows, width = q_ref.shape
-    local_len = k_ref.shape[1]
+    layers, local_len, width = k_ref.shape
+    rows = q_ref.shape[0] // SUBLANES
     fits, capacity = idx_ref.shape
     start = lax.axis_index("seq") * local_len
     lane = lax.broadcasted_iota(jnp.int32, (rows, LANES), 1)
     scale = width ** (-0.5)
     for layer in range(layers):
+        query_rows = q_ref[pl.ds(layer, rows, stride=SUBLANES), :].astype(jnp.bfloat16)
         scores = (
-            lax.dot_general(q_ref[layer], k_ref[layer], NT, preferred_element_type=jnp.float32)
+            lax.dot_general(query_rows, k_ref[layer], NT, preferred_element_type=jnp.float32)
             * scale
         )
         s_ref[layer] = scores
@@ -132,27 +133,171 @@
     return solve_rows(jnp.where(diagonal, gram + ridge, gram), target)
 
 
-def solve_kernel(sizes_ref, e_ref, aux_ref, p_ref, x_ref):
-    groups = e_ref.shape[0]
+def enter(axes):
+    barrier = pltpu.get_barrier_semaphore()
+    total = 0
+    for axis in axes:
+        me, size = lax.axis_index(axis), lax.axis_size(axis)
+        for step in range(1, size):
+            pl.semaphore_signal(
+                barrier, inc=1, device_id={axis: lax.rem(me + step, size)}, device_id_type=MESH
+            )
+        total += size - 1
+    pl.semaphore_wait(barrier, total)
+
+
+def send(source, target, send_sem, recv_sem, axis, peer):
+    return pltpu.make_async_remote_copy(
+        src_ref=source,
+        dst_ref=target,
+        send_sem=send_sem,
+        recv_sem=recv_sem,
+        device_id={axis: peer},
+        device_id_type=MESH,
+    )
+
+
+def query_kernel(q_ref, out_ref, piece, column, table, send_head, recv_head, send_seq, recv_seq):
+    layers, heads, count, width = q_ref.shape
+    my_head, my_seq = lax.axis_index("head"), lax.axis_index("seq")
+    groups = lax.axis_size("seq")
+    for head in range(heads):
+        for layer in range(layers):
+            piece[head, layer : layer + 1, :] = q_ref[layer, head].astype(jnp.float32)
+        piece[head, layers:, :] = jnp.zeros((SUBLANES - layers, width), jnp.float32)
+    enter(("head", "seq"))
+    column[0] = piece[my_head]
+    copies = []
+    for step in range(1, heads):
+        peer = lax.rem(my_head + step, heads)
+        copies.append(
+            send(
+                piece.at[peer],
+                column.at[step],
+                send_head.at[step],
+                recv_head.at[step],
+                "head",
+                peer,
+            )
+        )
+        copies[-1].start()
+    for copy in copies:
+        copy.wait_recv()
+    later = []
+    for step in range(1, groups):
+        peer = lax.rem(my_seq + step, groups)
+        later.append(
+            send(column, table.at[my_seq], send_seq.at[step], recv_seq.at[step], "seq", peer)
+        )
+        later[-1].start()
+    table[my_seq] = column[...]
+    for copy in copies:
+        copy.wait_send()
+    for copy in later:
+        copy.wait()
+    out_ref[...] = table[...]
+
+
+def solve_kernel(
+    sizes_ref, e_ref, aux_ref, p_ref, x_ref,
+    e_in, aux_in, p_all, x_all, p_mine, x_mine,
+    send_in, recv_in, send_out, recv_out,
+):
+    groups = lax.axis_size("seq")
+    me = lax.axis_index("seq")
     fits = sizes_ref.shape[1]
-    fit = jnp.minimum(lax.axis_index("seq"), fits - 1)
-    size = sizes_ref[0, fit].astype(jnp.float32)
-    probs, target = merge_fit(
-        lambda s: e_ref[s], lambda s, part: aux_ref[s, part], groups, size
-    )
-    p_ref[...] = probs
-    x_ref[...] = fit_rows(probs, target, size)
-
-
-def place_kernel(slot_ref, p_ref, x_ref, out_ref):
+    fit = jnp.minimum(me, fits - 1)
+
+    def only(condition, act):
+        if groups <= fits:
+            act()
+        else:
+            pl.when(condition)(act)
+
+    def inbound(step):
+        peer = lax.rem(me + step, groups)
+        target = jnp.minimum(peer, fits - 1)
+        return peer, [
+            send(
+                aux_ref.at[target], aux_in.at[step],
+                send_in.at[0, step], recv_in.at[0, step], "seq", peer,
+            ),
+            send(
+                e_ref.at[target], e_in.at[step],
+                send_in.at[1, step], recv_in.at[1, step], "seq", peer,
+            ),
+        ]
+
+    enter(("seq",))
+    moves = [inbound(step) for step in range(1, groups)]
+    for part in range(2):
+        for peer, pair in moves:
+            only(peer < fits, pair[part].start)
+    aux_in[0] = aux_ref[fit]
+    e_in[0] = e_ref[fit]
+
+    outs = []
+    for step in range(1, groups):
+        peer = lax.rem(me + step, groups)
+        outs.append(
+            [
+                send(
+                    p_mine, p_all.at[fit],
+                    send_out.at[0, step], recv_out.at[0, step], "seq", peer,
+                ),
+                send(
+                    x_mine, x_all.at[fit],
+                    send_out.at[1, step], recv_out.at[1, step], "seq", peer,
+                ),
+            ]
+        )
+
+    def work():
+        for peer, pair in moves:
+            pair[0].wait_recv()
+        for peer, pair in moves:
+            pair[1].wait_recv()
+        size = sizes_ref[0, fit].astype(jnp.float32)
+        probs, target = merge_fit(
+            lambda s: e_in[s], lambda s, part: aux_in[s, part], groups, size
+        )
+        p_mine[...] = probs
+        p_all[fit] = probs
+        for pair in outs:
+            pair[0].start()
+        solved = fit_rows(probs, target, size)
+        x_mine[...] = solved
+        x_all[fit] = solved
+        for pair in outs:
+            pair[1].start()
+
+    only(me < fits, work)
+    for step in range(1, groups):
+        source = lax.rem(me + groups - step, groups)
+        for part in range(2):
+            only(source < fits, outs[step - 1][part].wait_recv)
+            only(me < fits, outs[step - 1][part].wait_send)
+            only(moves[step - 1][0] < fits, moves[step - 1][1][part].wait_send)
+    p_ref[...] = p_all[...]
+    x_ref[...] = x_all[...]
+
+
+def place_kernel(owners_ref, p_ref, x_ref, out_ref):
+    me = lax.axis_index("seq")
+    fits = p_ref.shape[0]
+    count = jnp.int32(0)
+    chosen = [jnp.int32(0)] * SLOTS
+    for fit in range(fits):
+        mine = owners_ref[0, fit] == me
+        for slot in range(SLOTS):
+            chosen[slot] = jnp.where(mine & (count == slot), fit, chosen[slot])
+        count = count + mine.astype(jnp.int32)
     for slot in range(SLOTS):
-        fit = slot_ref[0, slot]
-        live = slot_ref[1, slot]
-
-        @pl.when(live > 0)
+
+        @pl.when(count > slot)
         def _():
-            probs = p_ref[fit]
-            rows = x_ref[fit]
+            probs = p_ref[chosen[slot]]
+            rows = x_ref[chosen[slot]]
             high = rows.astype(jnp.bfloat16)
             low = (rows - high.astype(jnp.float32)).astype(jnp.bfloat16)
             out_ref[0, slot] = lax.dot_general(
@@ -162,7 +307,7 @@
                 preferred_element_type=jnp.float32,
             ).astype(jnp.bfloat16)
 
-        @pl.when(live == 0)
+        @pl.when(count <= slot)
         def _():
             out_ref[0, slot] = jnp.zeros(out_ref.shape[2:], jnp.bfloat16)
 
@@ -173,15 +318,28 @@
 
 
 def on_device(queries, keys, values, indices, sizes, owners):
-    regrouped = lax.all_to_all(queries, "head", split_axis=1, concat_axis=2, tiled=True)
-    gathered = lax.all_gather(regrouped, "seq", axis=2, tiled=True)
-    all_queries = gathered[:, 0]
-    layers, rows, width = all_queries.shape
-    key_rows = keys[:, 0]
-    value_rows = values[:, 0]
-    local_len = key_rows.shape[1]
+    layers, heads, count, width = queries.shape
+    groups = lax.axis_size("seq")
+    rows = groups * heads * count
+    local_len = keys.shape[2]
     fits, capacity = indices.shape[1:]
-    groups = lax.axis_size("seq")
+    dma = pltpu.SemaphoreType.DMA
+    all_queries = pl.pallas_call(
+        query_kernel,
+        out_shape=jax.ShapeDtypeStruct((groups, heads, SUBLANES, width), jnp.float32),
+        in_specs=[VMEM],
+        out_specs=VMEM,
+        scratch_shapes=[
+            pltpu.VMEM((heads, SUBLANES, width), jnp.float32),
+            pltpu.VMEM((heads, SUBLANES, width), jnp.float32),
+            pltpu.VMEM((groups, heads, SUBLANES, width), jnp.float32),
+            dma((heads,)),
+            dma((heads,)),
+            dma((groups,)),
+            dma((groups,)),
+        ],
+        compiler_params=pltpu.CompilerParams(collective_id=1, has_side_effects=True, **PARAMS),
+    )(queries)
     expo, aux = pl.pallas_call(
         attend_kernel,
         out_shape=(
@@ -195,47 +353,42 @@
             pltpu.VMEM((rows, capacity), jnp.float32),
         ],
         compiler_params=pltpu.CompilerParams(**PARAMS),
-    )(sizes, all_queries, key_rows, value_rows, indices[0])
-    if groups > fits:
-        spare = groups - fits
-        expo = jnp.pad(expo, ((0, spare), (0, 0), (0, 0)))
-        aux = jnp.pad(aux, ((0, spare), (0, 0), (0, 0), (0, 0)))
-    expo = lax.all_to_all(expo, "seq", split_axis=0, concat_axis=0, tiled=True)
-    aux = lax.all_to_all(aux, "seq", split_axis=0, concat_axis=0, tiled=True)
+    )(
+        sizes,
+        all_queries.reshape(rows * SUBLANES, width),
+        keys[:, 0],
+        values[:, 0],
+        indices[0],
+    )
     probs, solved = pl.pallas_call(
         solve_kernel,
         out_shape=(
-            jax.ShapeDtypeStruct((rows, capacity), jnp.bfloat16),
-            jax.ShapeDtypeStruct((rows, width), jnp.float32),
+            jax.ShapeDtypeStruct((fits, rows, capacity), jnp.bfloat16),
+            jax.ShapeDtypeStruct((fits, rows, width), jnp.float32),
         ),
         in_specs=[SMEM] + [VMEM] * 2,
         out_specs=(VMEM, VMEM),
-        compiler_params=pltpu.CompilerParams(**PARAMS),
+        scratch_shapes=[
+            pltpu.VMEM((groups, rows, capacity), jnp.bfloat16),
+            pltpu.VMEM((groups, 2, rows, width), jnp.float32),
+            pltpu.VMEM((fits, rows, capacity), jnp.bfloat16),
+            pltpu.VMEM((fits, rows, width), jnp.float32),
+            pltpu.VMEM((rows, capacity), jnp.bfloat16),
+            pltpu.VMEM((rows, width), jnp.float32),
+            dma((2, groups)),
+            dma((2, groups)),
+            dma((2, groups)),
+            dma((2, groups)),
+        ],
+        compiler_params=pltpu.CompilerParams(collective_id=2, has_side_effects=True, **PARAMS),
     )(sizes, expo, aux)
-    probs = lax.all_gather(probs, "seq")[:fits]
-    solved = lax.all_gather(solved, "seq")[:fits]
-    return place(owners, probs, solved, capacity)
-
-
-def place(owners, probs, solved, capacity):
-    width = solved.shape[-1]
-    owned = owners[0]
-    fits = owned.shape[0]
-    fit_ids = jnp.arange(fits, dtype=jnp.int32)
-    same = owned[:, None] == owned[None, :]
-    earlier = jnp.sum((same & (fit_ids[:, None] > fit_ids[None, :])).astype(jnp.int32), axis=1)
-    match = (owned == lax.axis_index("seq"))[None, :] & (
-        earlier[None, :] == jnp.arange(SLOTS, dtype=jnp.int32)[:, None]
-    )
-    chosen = jnp.sum(jnp.where(match, fit_ids[None, :], 0), axis=1)
-    live = jnp.any(match, axis=1).astype(jnp.int32)
     return pl.pallas_call(
         place_kernel,
         out_shape=jax.ShapeDtypeStruct((1, SLOTS, capacity, width), jnp.bfloat16),
         in_specs=[SMEM, VMEM, VMEM],
         out_specs=VMEM,
         compiler_params=pltpu.CompilerParams(**PARAMS),
-    )(jnp.stack([chosen, live]), probs, solved)
+    )(owners, probs, solved)
 
 
 def solution(mesh):

time: 155 us -> 75.6 us (0.49)
  blocking collectives: 113 us -> 0 us
  Pallas kernels: 25.6 us -> 74 us
  waiting for transfers between devices: 8.56 us -> 0 us
  starting transfers between devices: 3.49 us -> 0 us
    all_gather x3 -> x0, blocking collectives: 92.8 us -> none  [the longest x1 33.4 us: on_device(): probs = lax.all_gather(probs, 'seq')[:fits]]
    pallas_call x2 -> x3, Pallas kernels: 7.2 us -> 55.6 us  [the longest x1 39.5 us: on_device(): pl.pallas_call(solve_kernel, out_shape=(jax.ShapeDtypeStruct((fits, rows,...]
    all_to_all x2 -> x0, blocking collectives: 20.1 us -> none  [the longest x1 12.3 us: on_device(): aux = lax.all_to_all(aux, 'seq', split_axis=0, concat_axis=0, tiled=True)]
    all_to_all x1 -> x0, waiting for transfers between devices: 8.56 us -> none  [on_device(): expo = lax.all_to_all(expo, 'seq', split_axis=0, concat_axis=0, tiled=True)]
    all_to_all x1 -> x0, starting transfers between devices: 3.49 us -> none  [on_device(): expo = lax.all_to_all(expo, 'seq', split_axis=0, concat_axis=0, tiled=True)]
  transfers between devices with their start and end apart: 1 -> 0, of which waited for: 1 -> 0; matrix products, arithmetic and copies ran while one was open for 1% -> 0% of each run, Pallas kernels for 0% -> 0%
where the time goes in v2:
time: 75.6 us; the launch traced here: 75.3 us
  Pallas kernels  74 us (98%)
  local copies, waits for them, and re-layouts  1.28 us (2%)
    pallas_call x1, Pallas kernels, on_device(): pl.pallas_call(solve_kernel, out_shape=(jax.ShapeDtypeStruct((fits, rows,...  39.5 us
    pallas_call x1, Pallas kernels, on_device(): pl.pallas_call(attend_kernel, out_shape=(jax.ShapeDtypeStruct((fits, rows...  18.4 us
    pallas_call x1, Pallas kernels, on_device(): pl.pallas_call(query_kernel, out_shape=jax.ShapeDtypeStruct((groups, head...  14 us
    pallas_call x1, Pallas kernels, on_device(): pl.pallas_call(place_kernel, out_shape=jax.ShapeDtypeStruct((1, SLOTS, ca...  2.11 us

profile of v2, /device:TPU:0, one launch (start us, length us, event | category | flops | bytes accessed | tf_op | source)
XLA Modules:
  0.0 75.3 jit_solution(4335874763080321115)
XLA Ops:
  0.0 0.0 copy-start
  0.0 0.7 copy-done
  0.7 0.6 copy.7.q_ref
  1.3 14.0 %shard_map.64 = f32[8,4,8,128]{3,2,1,0:T(8,128)} custom-call(bf16[2,4,1,128]{3,2,1,0:T(2,128)(2,1)} %copy.7.q_ref), custom_call_target="tpu_custom_call" | custom-call | tf_op jit(solution)/shard_map/pallas_call | solution.py:327
  15.3 18.4 %shard_map.65 = (bf16[8,32,1024]{2,1,0:T(8,128)(2,1)}, f32[8,2,32,128]{3,2,1,0:T(8,128)}) custom-call(s32[1,8]{1,0:T(1,128)} %sizes_ref.3, f32[256,128]{1,0:T(8,128)} %bitcast.6, bf16[2,2048,128]{2,1,0:T(8,128)(2,1)} %bitcast.4, bf16[2,2048,128]{2,1,0:T(8,128)(2,1)} %bitcast.5, s32[8,1024]{1,0:T(8,128)} %bitcast.7), custom_call_target="tpu_custom_call" | custom-call | tf_op jit(solution)/shard_map/pallas_call | solution.py:343
  33.7 39.5 %shard_map.66 = (bf16[8,32,1024]{2,1,0:T(8,128)(2,1)}, f32[8,32,128]{2,1,0:T(8,128)}) custom-call(s32[1,8]{1,0:T(1,128)} %sizes_ref.3, bf16[8,32,1024]{2,1,0:T(8,128)(2,1)} %get-tuple-element.9.e_ref, f32[8,2,32,128]{3,2,1,0:T(8,128)} %get-tuple-element.10.aux_ref), custom_call_target="tpu_custom_call" | custom-call | tf_op jit(solution)/shard_map/pallas_call | solution.py:363
  73.2 2.1 %shard_map.67 = bf16[1,3,1024,128]{3,2,1,0:T(8,128)(2,1)} custom-call(s32[1,8]{1,0:T(1,128)} %owners_ref.1, bf16[8,32,1024]{2,1,0:T(8,128)(2,1)} %get-tuple-element.11.p_ref, f32[8,32,128]{2,1,0:T(8,128)} %get-tuple-element.12.x_ref), custom_call_target="tpu_custom_call" | custom-call | tf_op jit(solution)/shard_map/pallas_call | solution.py:385
Async XLA Ops:
  0.0 0.7 copy-start

commit v3 on v2

v3 whole, which is shorter than its diff:
```python
import jax
import jax.numpy as jnp
from jax import lax
from jax.experimental import pallas as pl
from jax.experimental.pallas import tpu as pltpu
from jax.sharding import PartitionSpec as P

FITS_LAYER = 4
SLOTS = 3
RIDGE = 0.3
LANES = 128
FAR = -(2.0**100)
LOG2E = 1.4426950408889634
PAIR = 2

SUBLANES = 8
MESH = pl.DeviceIdType.MESH
NT = (((1,), (1,)), ((), ()))
TN = (((0,), (0,)), ((), ()))


def solve_rows(system, target, halfway):
    rows = system.shape[0]
    row = lax.broadcasted_iota(jnp.int32, (rows, 1), 0)
    if rows <= 64:
        for k in range(rows):
            if k == rows // 2:
                halfway()
            inverse = 1.0 / system[k : k + 1, k : k + 1]
            pivot_s = system[k : k + 1, :] * inverse
            pivot_t = target[k : k + 1, :] * inverse
            column = jnp.where(row == k, system[:, k : k + 1] - 1.0, system[:, k : k + 1])
            system = system - column * pivot_s
            target = target - column * pivot_t
        return target
    halfway()
    lane = lax.broadcasted_iota(jnp.int32, (1, rows), 1)

    def step(k, state):
        system, target = state
        column = jnp.sum(jnp.where(lane == k, system, 0.0), axis=1, keepdims=True)
        here = row == k
        inverse = 1.0 / jnp.sum(jnp.where(here, column, 0.0), axis=0, keepdims=True)
        pivot_s = jnp.sum(jnp.where(here, system, 0.0), axis=0, keepdims=True) * inverse
        pivot_t = jnp.sum(jnp.where(here, target, 0.0), axis=0, keepdims=True) * inverse
        column = jnp.where(here, column - 1.0, column)
        return system - column * pivot_s, target - column * pivot_t

    return lax.fori_loop(0, rows, step, (system, target))[1]


def split_exponent(block, capacity):
    tail = block[:, capacity:].astype(jnp.float32)
    return block[:, :capacity].astype(jnp.float32), tail[:, 0:1] + tail[:, 64:65]


def joined_exponent(expo, top, lane):
    high = top.astype(jnp.bfloat16)
    low = (top - high.astype(jnp.float32)).astype(jnp.bfloat16)
    tail = jnp.where(lane < 64, high.astype(jnp.float32), low.astype(jnp.float32))
    return jnp.concatenate([expo.astype(jnp.bfloat16), tail.astype(jnp.bfloat16)], axis=1)


def enter(axes):
    barrier = pltpu.get_barrier_semaphore()
    total = 0
    for axis in axes:
        me, size = lax.axis_index(axis), lax.axis_size(axis)
        for step in range(1, size):
            pl.semaphore_signal(
                barrier, inc=1, device_id={axis: lax.rem(me + step, size)}, device_id_type=MESH
            )
        total += size - 1
    pl.semaphore_wait(barrier, total)


def send(source, target, send_sem, recv_sem, axis, peer):
    return pltpu.make_async_remote_copy(
        src_ref=source,
        dst_ref=target,
        send_sem=send_sem,
        recv_sem=recv_sem,
        device_id={axis: peer},
        device_id_type=MESH,
    )


def query_kernel(q_ref, out_ref, piece, column, table, send_head, recv_head, send_seq, recv_seq):
    layers, heads, count, width = q_ref.shape
    my_head, my_seq = lax.axis_index("head"), lax.axis_index("seq")
    groups = lax.axis_size("seq")
    for head in range(heads):
        for layer in range(layers):
            piece[head, layer : layer + 1, :] = q_ref[layer, head].astype(jnp.float32)
        piece[head, layers:, :] = jnp.zeros((SUBLANES - layers, width), jnp.float32)
    enter(("head", "seq"))
    column[0] = piece[my_head]
    copies = []
    for step in range(1, heads):
        peer = lax.rem(my_head + step, heads)
        copies.append(
            send(
                piece.at[peer],
                column.at[step],
                send_head.at[step],
                recv_head.at[step],
                "head",
                peer,
            )
        )
        copies[-1].start()
    for copy in copies:
        copy.wait_recv()
    later = []
    for step in range(1, groups):
        peer = lax.rem(my_seq + step, groups)
        later.append(
            send(column, table.at[my_seq], send_seq.at[step], recv_seq.at[step], "seq", peer)
        )
        later[-1].start()
    table[my_seq] = column[...]
    for copy in copies:
        copy.wait_send()
    for copy in later:
        copy.wait()
    out_ref[...] = table[...]


def fit_kernel(
    sizes_ref, q_ref, k_ref, v_ref, idx_ref, p_ref, x_ref,
    s_ref, g_ref, part, part_in, chunk_mine, chunks, e_out, e_in, z_out, z_in,
    p_mine, p_all, x_mine, x_all,
    send_part, recv_part, send_chunk, recv_chunk, send_e, recv_e, send_z, recv_z,
    send_p, recv_p, send_f, recv_f, send_x, recv_x,
):
    layers, local_len, width = k_ref.shape
    rows = q_ref.shape[0] // SUBLANES
    fits, capacity = idx_ref.shape
    groups, me = lax.axis_size("seq"), lax.axis_index("seq")
    outer, inner = me // PAIR, lax.rem(me, PAIR)
    outers, half = groups // PAIR, fits // PAIR
    partner = outer * PAIR + 1 - inner
    fit_mine = jnp.minimum(me, fits - 1)
    chunk = layers * rows // groups
    start = me * local_len
    lane = lax.broadcasted_iota(jnp.int32, (rows, LANES), 1)
    exact = outers == half

    for layer in range(layers):
        query_rows = q_ref[pl.ds(layer, rows, stride=SUBLANES), :].astype(jnp.bfloat16)
        scores = lax.dot_general(
            query_rows, k_ref[layer], NT, preferred_element_type=jnp.float32
        ) * (width ** (-0.5) * LOG2E)
        s_ref[layer] = scores
        peak = jnp.max(scores, axis=1, keepdims=True)
        weights = jnp.exp2(scores - peak)
        total = jnp.sum(weights, axis=1, keepdims=True)
        numer = jnp.dot(
            weights.astype(jnp.bfloat16), v_ref[layer], preferred_element_type=jnp.float32
        )
        side = jnp.where(lane < 64, total, peak)
        for piece in range(rows // chunk):
            slot = layer * (rows // chunk) + piece
            part[slot, 0] = numer[piece * chunk : (piece + 1) * chunk]
            part[slot, 1] = side[piece * chunk : (piece + 1) * chunk]

    def produce(fit):
        layer = fit // FITS_LAYER
        size = sizes_ref[0, fit]

        def one_tile(tile, top):
            base = pl.multiple_of(tile * LANES, LANES)
            drawn = idx_ref[:, pl.ds(base, LANES)]
            mine = lax.broadcasted_iota(jnp.int32, (fits, LANES), 0) == fit
            offset = jnp.sum(jnp.where(mine, drawn, 0), axis=0, keepdims=True) - start
            column = base + lax.broadcasted_iota(jnp.int32, (1, LANES), 1)
            inside = (offset >= 0) & (offset < local_len) & (column < size)
            offset = jnp.broadcast_to(jnp.where(inside, offset, -1), (rows, LANES))
            high = offset >> 7
            low = offset & (LANES - 1)
            picked = jnp.full((rows, LANES), FAR, jnp.float32)
            for block in range(local_len // LANES):
                piece = s_ref[layer, :, block * LANES : (block + 1) * LANES]
                found = jnp.take_along_axis(piece, low, axis=1, mode="promise_in_bounds")
                picked = jnp.where(high == block, found, picked)
            g_ref[:, pl.ds(base, LANES)] = picked
            return jnp.maximum(top, jnp.max(picked, axis=1, keepdims=True))

        top = lax.fori_loop(
            0, capacity // LANES, one_tile, jnp.full((rows, 1), FAR, jnp.float32)
        )
        top = jnp.ceil(top)
        picked = g_ref[...]
        return jnp.where(picked > 0.5 * FAR, jnp.exp2(picked - top), 0.0), top

    enter(("seq",))
    parts = []
    for step in range(1, groups):
        peer = lax.rem(me + step, groups)
        parts.append(
            send(
                part.at[peer], part_in.at[step],
                send_part.at[step], recv_part.at[step], "seq", peer,
            )
        )
        parts[-1].start()
    part_in[0] = part[me]

    def column_of(j):
        return lax.rem(outer + 1 + j, outers) if exact else jnp.int32(j)

    across = []
    for j in range(half):
        expo, top = produce(column_of(j) * PAIR + 1 - inner)
        e_out[j] = joined_exponent(expo, top, lane)
        across.append(
            send(e_out.at[j], e_in.at[j], send_e.at[j], recv_e.at[j], "seq", partner)
        )
        if j > 0:
            across[j - 1].start()

    for copy in parts:
        copy.wait_recv()
    peak = part_in[0, 1][:, 64:65]
    for step in range(1, groups):
        peak = jnp.maximum(peak, part_in[step, 1][:, 64:65])
    numer, total = 0.0, 0.0
    for step in range(groups):
        factor = jnp.exp2(part_in[step, 1][:, 64:65] - peak)
        numer = numer + part_in[step, 0] * factor
        total = total + part_in[step, 1][:, 0:1] * factor
    merged = numer / total
    chunk_mine[...] = merged
    chunks[me] = merged
    across[half - 1].start()

    down, spread = [], []
    for j in range(half):
        dest = column_of(j)
        expo, top = produce(dest * PAIR + inner)
        if j == 0:
            for step in range(1, groups):
                peer = lax.rem(me + step, groups)
                spread.append(
                    send(
                        chunk_mine, chunks.at[me],
                        send_chunk.at[step], recv_chunk.at[step], "seq", peer,
                    )
                )
                spread[-1].start()
        across[j].wait_recv()
        other, other_top = split_exponent(e_in[j], capacity)
        both = jnp.maximum(top, other_top)
        expo = expo * jnp.exp2(top - both) + other * jnp.exp2(other_top - both)
        block = joined_exponent(expo, both, lane)
        copy = send(
            z_out.at[j], z_in.at[outer], send_z.at[j], recv_z.at[outer],
            "seq", dest * PAIR + inner,
        )
        down.append((dest, copy))
        if exact:
            if j == half - 1:
                z_in[outer] = block
            else:
                z_out[j] = block
                copy.start()
        else:
            z_out[j] = block
            pl.when(dest != outer)(copy.start)

            @pl.when(dest == outer)
            def _():
                z_in[outer] = block

    def only(condition, act):
        if exact:
            act()
        else:
            pl.when(condition)(act)

    def source_z(step):
        source = lax.rem(outer + step, outers)
        return source, send(
            z_out.at[0], z_in.at[source], send_z.at[0], recv_z.at[source], "seq", partner
        )

    def gave_p(step, target):
        return send(
            p_mine, p_all.at[fit_mine], send_p.at[step], recv_p.at[outer],
            "seq", target * PAIR + inner,
        )

    def came_p(source):
        fit = jnp.minimum(source, half - 1) * PAIR + inner
        arrival = send(
            p_mine, p_all.at[fit], send_p.at[0], recv_p.at[source], "seq", partner
        )
        onward = send(
            p_all.at[fit], p_all.at[fit], send_f.at[source], recv_f.at[source], "seq", partner
        )
        return arrival, onward

    def back_p(source):
        fit = jnp.minimum(source, half - 1) * PAIR + 1 - inner
        return send(
            p_mine, p_all.at[fit], send_f.at[source], recv_f.at[source], "seq", partner
        )

    gifts = [gave_p(step, lax.rem(outer + step, outers)) for step in range(1, outers)]
    own_onward = send(
        p_mine, p_all.at[fit_mine], send_f.at[outer], recv_f.at[outer], "seq", partner
    )
    results = [
        send(
            x_mine, x_all.at[fit_mine], send_x.at[step], recv_x.at[step],
            "seq", lax.rem(me + step, groups),
        )
        for step in range(1, groups)
    ]

    def relay():
        for step in range(1, outers):
            source = lax.rem(outer + outers - step, outers)
            arrival, onward = came_p(source)

            def pass_on():
                arrival.wait_recv()
                onward.start()

            only(source < half, pass_on)

    for copy in spread:
        copy.wait_recv()

    def work():
        for step in range(1, outers):
            source_z(step)[1].wait_recv()
        blocks = [split_exponent(z_in[source], capacity) for source in range(outers)]
        top = blocks[0][1]
        for _, other in blocks[1:]:
            top = jnp.maximum(top, other)
        probs = 0.0
        for expo, other in blocks:
            probs = probs + expo * jnp.exp2(other - top)
        probs = (probs / jnp.sum(probs, axis=1, keepdims=True)).astype(jnp.bfloat16)
        p_mine[...] = probs
        p_all[fit_mine] = probs
        gram = lax.dot_general(probs, probs, NT, preferred_element_type=jnp.float32)
        for copy in gifts:
            copy.start()
        own_onward.start()
        diagonal = lax.broadcasted_iota(jnp.int32, (rows, rows), 0) == lax.broadcasted_iota(
            jnp.int32, (rows, rows), 1
        )
        trace = jnp.sum(jnp.where(diagonal, gram, 0.0))
        ridge = RIDGE * trace / sizes_ref[0, fit_mine].astype(jnp.float32)
        span = rows // chunk
        first = (fit_mine // FITS_LAYER) * span
        target = jnp.concatenate([chunks[first + piece] for piece in range(span)], axis=0)
        target = target.astype(jnp.bfloat16).astype(jnp.float32)
        solved = solve_rows(
            jnp.where(diagonal, gram + ridge, gram), target, relay if exact else lambda: None
        )
        x_mine[...] = solved
        x_all[fit_mine] = solved
        for copy in results:
            copy.start()

    only(outer < half, work)
    if not exact:
        relay()
    for copy in parts + spread + across:
        copy.wait_send()
    for j in range(half):
        dest, copy = down[j]
        if exact:
            if j < half - 1:
                copy.wait_send()
        else:
            pl.when(dest != outer)(copy.wait_send)
    for step in range(1, outers):
        source = lax.rem(outer + outers - step, outers)
        only(outer < half, gifts[step - 1].wait_send)
        only(source < half, came_p(source)[1].wait_send)
    only(outer < half, own_onward.wait_send)
    for source in range(half):
        back_p(source).wait_recv()
    for step in range(1, groups):
        source = lax.rem(me + groups - step, groups)
        only(source < fits, results[step - 1].wait_recv)
        only(outer < half, results[step - 1].wait_send)
    p_ref[...] = p_all[...]
    x_ref[...] = x_all[...]


def place_kernel(owners_ref, p_ref, x_ref, out_ref):
    me = lax.axis_index("seq")
    fits = p_ref.shape[0]
    count = jnp.int32(0)
    chosen = [jnp.int32(0)] * SLOTS
    for fit in range(fits):
        mine = owners_ref[0, fit] == me
        for slot in range(SLOTS):
            chosen[slot] = jnp.where(mine & (count == slot), fit, chosen[slot])
        count = count + mine.astype(jnp.int32)
    for slot in range(SLOTS):

        @pl.when(count > slot)
        def _():
            probs = p_ref[chosen[slot]]
            rows = x_ref[chosen[slot]]
            high = rows.astype(jnp.bfloat16)
            low = (rows - high.astype(jnp.float32)).astype(jnp.bfloat16)
            out_ref[0, slot] = lax.dot_general(
                jnp.concatenate([probs, probs], axis=0),
                jnp.concatenate([high, low], axis=0),
                TN,
                preferred_element_type=jnp.float32,
            ).astype(jnp.bfloat16)

        @pl.when(count <= slot)
        def _():
            out_ref[0, slot] = jnp.zeros(out_ref.shape[2:], jnp.bfloat16)


VMEM = pl.BlockSpec(memory_space=pltpu.VMEM)
SMEM = pl.BlockSpec(memory_space=pltpu.SMEM)
PARAMS = dict(vmem_limit_bytes=60 * 1024 * 1024)


def on_device(queries, keys, values, indices, sizes, owners):
    layers, heads, count, width = queries.shape
    groups = lax.axis_size("seq")
    rows = groups * heads * count
    local_len = keys.shape[2]
    fits, capacity = indices.shape[1:]
    dma = pltpu.SemaphoreType.DMA
    all_queries = pl.pallas_call(
        query_kernel,
        out_shape=jax.ShapeDtypeStruct((groups, heads, SUBLANES, width), jnp.float32),
        in_specs=[VMEM],
        out_specs=VMEM,
        scratch_shapes=[
            pltpu.VMEM((heads, SUBLANES, width), jnp.float32),
            pltpu.VMEM((heads, SUBLANES, width), jnp.float32),
            pltpu.VMEM((groups, heads, SUBLANES, width), jnp.float32),
            dma((heads,)),
            dma((heads,)),
            dma((groups,)),
            dma((groups,)),
        ],
        compiler_params=pltpu.CompilerParams(collective_id=1, has_side_effects=True, **PARAMS),
    )(queries)
    outers, half = groups // PAIR, fits // PAIR
    chunk = layers * rows // groups
    packed = (rows, capacity + LANES)
    probs, solved = pl.pallas_call(
        fit_kernel,
        out_shape=(
            jax.ShapeDtypeStruct((fits, rows, capacity), jnp.bfloat16),
            jax.ShapeDtypeStruct((fits, rows, width), jnp.float32),
        ),
        in_specs=[SMEM] + [VMEM] * 4,
        out_specs=(VMEM, VMEM),
        scratch_shapes=[
            pltpu.VMEM((layers, rows, local_len), jnp.float32),
            pltpu.VMEM((rows, capacity), jnp.float32),
            pltpu.VMEM((groups, 2, chunk, width), jnp.float32),
            pltpu.VMEM((groups, 2, chunk, width), jnp.float32),
            pltpu.VMEM((chunk, width), jnp.float32),
            pltpu.VMEM((groups, chunk, width), jnp.float32),
            pltpu.VMEM((half,) + packed, jnp.bfloat16),
            pltpu.VMEM((half,) + packed, jnp.bfloat16),
            pltpu.VMEM((half,) + packed, jnp.bfloat16),
            pltpu.VMEM((outers,) + packed, jnp.bfloat16),
            pltpu.VMEM((rows, capacity), jnp.bfloat16),
            pltpu.VMEM((fits, rows, capacity), jnp.bfloat16),
            pltpu.VMEM((rows, width), jnp.float32),
            pltpu.VMEM((fits, rows, width), jnp.float32),
            dma((groups,)),
            dma((groups,)),
            dma((groups,)),
            dma((groups,)),
            dma((half,)),
            dma((half,)),
            dma((half,)),
            dma((outers,)),
            dma((outers,)),
            dma((outers,)),
            dma((outers,)),
            dma((outers,)),
            dma((groups,)),
            dma((groups,)),
        ],
        compiler_params=pltpu.CompilerParams(collective_id=2, has_side_effects=True, **PARAMS),
    )(
        sizes,
        all_queries.reshape(rows * SUBLANES, width),
        keys[:, 0],
        values[:, 0],
        indices[0],
    )
    return pl.pallas_call(
        place_kernel,
        out_shape=jax.ShapeDtypeStruct((1, SLOTS, capacity, width), jnp.bfloat16),
        in_specs=[SMEM, VMEM, VMEM],
        out_specs=VMEM,
        compiler_params=pltpu.CompilerParams(**PARAMS),
    )(owners, probs, solved)


def solution(mesh):
    in_specs = (
        P(None, None, ("head", "seq"), None),
        P(None, "head", "seq", None),
        P(None, "head", "seq", None),
        P("head", None, None),
        P("head", None),
        P("head", None),
    )
    out_specs = P("head", "seq", None, None)
    return jax.shard_map(
        on_device, mesh=mesh, in_specs=in_specs, out_specs=out_specs, check_vma=False
    )
```

time: 75.6 us -> 57.4 us (0.76)
  Pallas kernels: 74 us -> 55.9 us
    pallas_call x2 -> x1, Pallas kernels: 57.8 us -> 39.5 us  [on_device(): pl.pallas_call(fit_kernel, out_shape=(jax.ShapeDtypeStruct((fits, rows, c...]
where the time goes in v3:
time: 57.4 us; the launch traced here: 57.2 us
  Pallas kernels  55.9 us (97%)
  local copies, waits for them, and re-layouts  1.28 us (2%)
    pallas_call x1, Pallas kernels, on_device(): pl.pallas_call(fit_kernel, out_shape=(jax.ShapeDtypeStruct((fits, rows, c...  39.5 us
    pallas_call x1, Pallas kernels, on_device(): pl.pallas_call(query_kernel, out_shape=jax.ShapeDtypeStruct((groups, head...  14 us
    pallas_call x1, Pallas kernels, on_device(): pl.pallas_call(place_kernel, out_shape=jax.ShapeDtypeStruct((1, SLOTS, ca...  2.33 us
    unnamed x3, local copies, waits for them, and re-layouts  1.28 us

profile of v3, /device:TPU:0, one launch (start us, length us, event | category | flops | bytes accessed | tf_op | source)
XLA Modules:
  0.0 57.2 jit_solution(8491507581500882468)
XLA Ops:
  0.0 0.0 copy-start
  0.0 0.7 %copy-done = bf16[2,4,1,128]{3,1,2,0:T(4,128)(2,1)S(1)} copy-done((bf16[2,4,1,128]{3,1,2,0:T(4,128)(2,1)S(1)}, bf16[2,4,1,128]{3,1,2,0:T(4,128)(2,1)}, u32[]{:S(2)}) %copy-start) | copy-done | bytes 2072
  0.7 0.6 %copy.7.q_ref = bf16[2,4,1,128]{3,2,1,0:T(2,128)(2,1)} copy(bf16[2,4,1,128]{3,1,2,0:T(4,128)(2,1)S(1)} %copy-done) | data formatting | bytes 4096 | tf_op args[0]
  1.3 14.0 %shard_map.64 = f32[8,4,8,128]{3,2,1,0:T(8,128)} custom-call(bf16[2,4,1,128]{3,2,1,0:T(2,128)(2,1)} %copy.7.q_ref), custom_call_target="tpu_custom_call" | custom-call | tf_op jit(solution)/shard_map/pallas_call | solution.py:438
  15.3 39.5 %shard_map.65 = (bf16[8,32,1024]{2,1,0:T(8,128)(2,1)}, f32[8,32,128]{2,1,0:T(8,128)}) custom-call(s32[1,8]{1,0:T(1,128)} %sizes_ref.1, f32[256,128]{1,0:T(8,128)} %bitcast.6, bf16[2,2048,128]{2,1,0:T(8,128)(2,1)} %bitcast.4, bf16[2,2048,128]{2,1,0:T(8,128)(2,1)} %bitcast.5, s32[8,1024]{1,0:T(8,128)} %bitcast.7), custom_call_target="tpu_custom_call" | custom-call | tf_op jit(solution)/shard_map/pallas_call | solution.py:457
  54.9 2.3 %shard_map.66 = bf16[1,3,1024,128]{3,2,1,0:T(8,128)(2,1)} custom-call(s32[1,8]{1,0:T(1,128)} %owners_ref.1, bf16[8,32,1024]{2,1,0:T(8,128)(2,1)} %get-tuple-element.7.p_ref, f32[8,32,128]{2,1,0:T(8,128)} %get-tuple-element.8.x_ref), custom_call_target="tpu_custom_call" | custom-call | tf_op jit(solution)/shard_map/pallas_call | solution.py:503
Async XLA Ops:
  0.0 0.7 %copy-start = (bf16[2,4,1,128]{3,1,2,0:T(4,128)(2,1)S(1)}, bf16[2,4,1,128]{3,1,2,0:T(4,128)(2,1)}, u32[]{:S(2)}) copy-start(bf16[2,4,1,128]{3,1,2,0:T(4,128)(2,1)} %param.6) | copy-start | bytes 6148

commit v4 on v3

--- a/solution.py
+++ b/solution.py
@@ -19,13 +19,11 @@
 TN = (((0,), (0,)), ((), ()))
 
 
-def solve_rows(system, target, halfway):
+def solve_rows(system, target):
     rows = system.shape[0]
     row = lax.broadcasted_iota(jnp.int32, (rows, 1), 0)
     if rows <= 64:
         for k in range(rows):
-            if k == rows // 2:
-                halfway()
             inverse = 1.0 / system[k : k + 1, k : k + 1]
             pivot_s = system[k : k + 1, :] * inverse
             pivot_t = target[k : k + 1, :] * inverse
@@ -33,7 +31,6 @@
             system = system - column * pivot_s
             target = target - column * pivot_t
         return target
-    halfway()
     lane = lax.broadcasted_iota(jnp.int32, (1, rows), 1)
 
     def step(k, state):
@@ -85,58 +82,18 @@
     )
 
 
-def query_kernel(q_ref, out_ref, piece, column, table, send_head, recv_head, send_seq, recv_seq):
-    layers, heads, count, width = q_ref.shape
-    my_head, my_seq = lax.axis_index("head"), lax.axis_index("seq")
-    groups = lax.axis_size("seq")
-    for head in range(heads):
-        for layer in range(layers):
-            piece[head, layer : layer + 1, :] = q_ref[layer, head].astype(jnp.float32)
-        piece[head, layers:, :] = jnp.zeros((SUBLANES - layers, width), jnp.float32)
-    enter(("head", "seq"))
-    column[0] = piece[my_head]
-    copies = []
-    for step in range(1, heads):
-        peer = lax.rem(my_head + step, heads)
-        copies.append(
-            send(
-                piece.at[peer],
-                column.at[step],
-                send_head.at[step],
-                recv_head.at[step],
-                "head",
-                peer,
-            )
-        )
-        copies[-1].start()
-    for copy in copies:
-        copy.wait_recv()
-    later = []
-    for step in range(1, groups):
-        peer = lax.rem(my_seq + step, groups)
-        later.append(
-            send(column, table.at[my_seq], send_seq.at[step], recv_seq.at[step], "seq", peer)
-        )
-        later[-1].start()
-    table[my_seq] = column[...]
-    for copy in copies:
-        copy.wait_send()
-    for copy in later:
-        copy.wait()
-    out_ref[...] = table[...]
-
-
 def fit_kernel(
-    sizes_ref, q_ref, k_ref, v_ref, idx_ref, p_ref, x_ref,
-    s_ref, g_ref, part, part_in, chunk_mine, chunks, e_out, e_in, z_out, z_in,
+    sizes_ref, q_in, k_hbm, v_hbm, idx_ref, p_ref, x_ref,
+    piece, column, table, k_ref, v_ref, s_ref, g_ref, part, part_in, chunk_mine, chunks, e_out, e_in, z_out, z_in,
     p_mine, p_all, x_mine, x_all,
-    send_part, recv_part, send_chunk, recv_chunk, send_e, recv_e, send_z, recv_z,
+    load, send_head, recv_head, send_seq, recv_seq, send_part, recv_part, send_chunk, recv_chunk, send_e, recv_e, send_z, recv_z,
     send_p, recv_p, send_f, recv_f, send_x, recv_x,
 ):
     layers, local_len, width = k_ref.shape
-    rows = q_ref.shape[0] // SUBLANES
     fits, capacity = idx_ref.shape
+    heads, my_head = lax.axis_size("head"), lax.axis_index("head")
     groups, me = lax.axis_size("seq"), lax.axis_index("seq")
+    rows = groups * heads
     outer, inner = me // PAIR, lax.rem(me, PAIR)
     outers, half = groups // PAIR, fits // PAIR
     partner = outer * PAIR + 1 - inner
@@ -146,8 +103,51 @@
     lane = lax.broadcasted_iota(jnp.int32, (rows, LANES), 1)
     exact = outers == half
 
+    loads = [
+        pltpu.make_async_copy(k_hbm, k_ref, load.at[0]),
+        pltpu.make_async_copy(v_hbm, v_ref, load.at[1]),
+    ]
+    for copy in loads:
+        copy.start()
+    drawn_rows = q_in[...].astype(jnp.float32)
+    for head in range(heads):
+        for layer in range(layers):
+            at = layer * heads + head
+            piece[head, layer : layer + 1, :] = drawn_rows[at : at + 1]
+        piece[head, layers:, :] = jnp.zeros((SUBLANES - layers, width), jnp.float32)
+    enter(("head", "seq"))
+    near = heads * SUBLANES
+    column[pl.ds(pl.multiple_of(my_head * SUBLANES, SUBLANES), SUBLANES), :] = piece[my_head]
+    first, second = [], []
+    for step in range(1, heads):
+        peer = lax.rem(my_head + step, heads)
+        first.append(
+            send(
+                piece.at[peer],
+                column.at[pl.ds(pl.multiple_of(my_head * SUBLANES, SUBLANES), SUBLANES), :],
+                send_head.at[step], recv_head.at[step], "head", peer,
+            )
+        )
+        first[-1].start()
+    for copy in first:
+        copy.wait_recv()
+    for step in range(1, groups):
+        peer = lax.rem(me + step, groups)
+        second.append(
+            send(
+                column, table.at[pl.ds(pl.multiple_of(me * near, near), near), :],
+                send_seq.at[step], recv_seq.at[step], "seq", peer,
+            )
+        )
+        second[-1].start()
+    table[pl.ds(pl.multiple_of(me * near, near), near), :] = column[...]
+    for copy in second:
+        copy.wait_recv()
+    for copy in loads:
+        copy.wait()
+
     for layer in range(layers):
-        query_rows = q_ref[pl.ds(layer, rows, stride=SUBLANES), :].astype(jnp.bfloat16)
+        query_rows = table[pl.ds(layer, rows, stride=SUBLANES), :].astype(jnp.bfloat16)
         scores = lax.dot_general(
             query_rows, k_ref[layer], NT, preferred_element_type=jnp.float32
         ) * (width ** (-0.5) * LOG2E)
@@ -159,10 +159,10 @@
             weights.astype(jnp.bfloat16), v_ref[layer], preferred_element_type=jnp.float32
         )
         side = jnp.where(lane < 64, total, peak)
-        for piece in range(rows // chunk):
-            slot = layer * (rows // chunk) + piece
-            part[slot, 0] = numer[piece * chunk : (piece + 1) * chunk]
-            part[slot, 1] = side[piece * chunk : (piece + 1) * chunk]
+        for at in range(rows // chunk):
+            slot = layer * (rows // chunk) + at
+            part[slot, 0] = numer[at * chunk : (at + 1) * chunk]
+            part[slot, 1] = side[at * chunk : (at + 1) * chunk]
 
     def produce(fit):
         layer = fit // FITS_LAYER
@@ -180,20 +180,23 @@
             low = offset & (LANES - 1)
             picked = jnp.full((rows, LANES), FAR, jnp.float32)
             for block in range(local_len // LANES):
-                piece = s_ref[layer, :, block * LANES : (block + 1) * LANES]
-                found = jnp.take_along_axis(piece, low, axis=1, mode="promise_in_bounds")
+                scored = s_ref[layer, :, block * LANES : (block + 1) * LANES]
+                found = jnp.take_along_axis(scored, low, axis=1, mode="promise_in_bounds")
                 picked = jnp.where(high == block, found, picked)
             g_ref[:, pl.ds(base, LANES)] = picked
             return jnp.maximum(top, jnp.max(picked, axis=1, keepdims=True))
 
         top = lax.fori_loop(
-            0, capacity // LANES, one_tile, jnp.full((rows, 1), FAR, jnp.float32)
+            0,
+            capacity // LANES,
+            one_tile,
+            jnp.full((rows, 1), FAR, jnp.float32),
+            unroll=4 if rows <= 64 else 1,
         )
         top = jnp.ceil(top)
         picked = g_ref[...]
         return jnp.where(picked > 0.5 * FAR, jnp.exp2(picked - top), 0.0), top
 
-    enter(("seq",))
     parts = []
     for step in range(1, groups):
         peer = lax.rem(me + step, groups)
@@ -355,21 +358,18 @@
         trace = jnp.sum(jnp.where(diagonal, gram, 0.0))
         ridge = RIDGE * trace / sizes_ref[0, fit_mine].astype(jnp.float32)
         span = rows // chunk
-        first = (fit_mine // FITS_LAYER) * span
-        target = jnp.concatenate([chunks[first + piece] for piece in range(span)], axis=0)
+        base = (fit_mine // FITS_LAYER) * span
+        target = jnp.concatenate([chunks[base + at] for at in range(span)], axis=0)
         target = target.astype(jnp.bfloat16).astype(jnp.float32)
-        solved = solve_rows(
-            jnp.where(diagonal, gram + ridge, gram), target, relay if exact else lambda: None
-        )
+        solved = solve_rows(jnp.where(diagonal, gram + ridge, gram), target)
         x_mine[...] = solved
         x_all[fit_mine] = solved
         for copy in results:
             copy.start()
 
     only(outer < half, work)
-    if not exact:
-        relay()
-    for copy in parts + spread + across:
+    relay()
+    for copy in first + second + parts + spread + across:
         copy.wait_send()
     for j in range(half):
         dest, copy = down[j]
@@ -424,6 +424,7 @@
 
 
 VMEM = pl.BlockSpec(memory_space=pltpu.VMEM)
+ANY = pl.BlockSpec(memory_space=pl.ANY)
 SMEM = pl.BlockSpec(memory_space=pltpu.SMEM)
 PARAMS = dict(vmem_limit_bytes=60 * 1024 * 1024)
 
@@ -435,22 +436,6 @@
     local_len = keys.shape[2]
     fits, capacity = indices.shape[1:]
     dma = pltpu.SemaphoreType.DMA
-    all_queries = pl.pallas_call(
-        query_kernel,
-        out_shape=jax.ShapeDtypeStruct((groups, heads, SUBLANES, width), jnp.float32),
-        in_specs=[VMEM],
-        out_specs=VMEM,
-        scratch_shapes=[
-            pltpu.VMEM((heads, SUBLANES, width), jnp.float32),
-            pltpu.VMEM((heads, SUBLANES, width), jnp.float32),
-            pltpu.VMEM((groups, heads, SUBLANES, width), jnp.float32),
-            dma((heads,)),
-            dma((heads,)),
-            dma((groups,)),
-            dma((groups,)),
-        ],
-        compiler_params=pltpu.CompilerParams(collective_id=1, has_side_effects=True, **PARAMS),
-    )(queries)
     outers, half = groups // PAIR, fits // PAIR
     chunk = layers * rows // groups
     packed = (rows, capacity + LANES)
@@ -460,9 +445,14 @@
             jax.ShapeDtypeStruct((fits, rows, capacity), jnp.bfloat16),
             jax.ShapeDtypeStruct((fits, rows, width), jnp.float32),
         ),
-        in_specs=[SMEM] + [VMEM] * 4,
+        in_specs=[SMEM, VMEM, ANY, ANY, VMEM],
         out_specs=(VMEM, VMEM),
         scratch_shapes=[
+            pltpu.VMEM((heads, SUBLANES, width), jnp.float32),
+            pltpu.VMEM((heads * SUBLANES, width), jnp.float32),
+            pltpu.VMEM((rows * SUBLANES, width), jnp.float32),
+            pltpu.VMEM((layers, local_len, width), jnp.bfloat16),
+            pltpu.VMEM((layers, local_len, width), jnp.bfloat16),
             pltpu.VMEM((layers, rows, local_len), jnp.float32),
             pltpu.VMEM((rows, capacity), jnp.float32),
             pltpu.VMEM((groups, 2, chunk, width), jnp.float32),
@@ -477,6 +467,11 @@
             pltpu.VMEM((fits, rows, capacity), jnp.bfloat16),
             pltpu.VMEM((rows, width), jnp.float32),
             pltpu.VMEM((fits, rows, width), jnp.float32),
+            dma((2,)),
+            dma((heads,)),
+            dma((heads,)),
+            dma((groups,)),
+            dma((groups,)),
             dma((groups,)),
             dma((groups,)),
             dma((groups,)),
@@ -495,7 +490,7 @@
         compiler_params=pltpu.CompilerParams(collective_id=2, has_side_effects=True, **PARAMS),
     )(
         sizes,
-        all_queries.reshape(rows * SUBLANES, width),
+        queries.reshape(layers * heads, width),
         keys[:, 0],
         values[:, 0],
         indices[0],

time: 57.4 us -> 46.9 us (0.82)
  Pallas kernels: 55.9 us -> 46.2 us
  local copies, waits for them, and re-layouts: 1.28 us -> 0 us
    pallas_call x1 -> x0, Pallas kernels: 14 us -> none  [on_device(): pl.pallas_call(query_kernel, out_shape=jax.ShapeDtypeStruct((groups, head...]
    pallas_call x1, Pallas kernels: 39.5 us -> 44.1 us  [on_device(): pl.pallas_call(fit_kernel, out_shape=(jax.ShapeDtypeStruct((fits, rows, c...]
    unnamed x3 -> x0, local copies, waits for them, and re-layouts: 1.28 us -> none
where the time goes in v4:
time: 46.9 us; the launch traced here: 46.2 us
  Pallas kernels  46.2 us (99%)
    pallas_call x1, Pallas kernels, on_device(): pl.pallas_call(fit_kernel, out_shape=(jax.ShapeDtypeStruct((fits, rows, c...  44.1 us
    pallas_call x1, Pallas kernels, on_device(): pl.pallas_call(place_kernel, out_shape=jax.ShapeDtypeStruct((1, SLOTS, ca...  2.11 us

profile of v4, /device:TPU:0, one launch (start us, length us, event | category | flops | bytes accessed | tf_op | source)
XLA Modules:
  0.0 46.2 jit_solution(1926495467496724335)
XLA Ops:
  0.0 44.1 %shard_map.64 = (bf16[8,32,1024]{2,1,0:T(8,128)(2,1)}, f32[8,32,128]{2,1,0:T(8,128)}) custom-call(s32[1,8]{1,0:T(1,128)} %sizes_ref.1, bf16[8,128]{1,0:T(8,128)(2,1)} %bitcast.7, bf16[2,2048,128]{2,1,0:T(8,128)(2,1)} %bitcast.4, bf16[2,2048,128]{2,1,0:T(8,128)(2,1)} %bitcast.5, s32[8,1024]{1,0:T(8,128)} %bitcast.6), custom_call_target="tpu_custom_call" | custom-call | tf_op jit(solution)/shard_map/pallas_call | solution.py:442
  44.1 2.1 %shard_map.65 = bf16[1,3,1024,128]{3,2,1,0:T(8,128)(2,1)} custom-call(s32[1,8]{1,0:T(1,128)} %owners_ref.1, bf16[8,32,1024]{2,1,0:T(8,128)(2,1)} %get-tuple-element.7.p_ref, f32[8,32,128]{2,1,0:T(8,128)} %get-tuple-element.8.x_ref), custom_call_target="tpu_custom_call" | custom-call | tf_op jit(solution)/shard_map/pallas_call | solution.py:498

commit v5 on v4

--- a/solution.py
+++ b/solution.py
@@ -191,7 +191,7 @@
             capacity // LANES,
             one_tile,
             jnp.full((rows, 1), FAR, jnp.float32),
-            unroll=4 if rows <= 64 else 1,
+            unroll=8 if rows <= 64 else 1,
         )
         top = jnp.ceil(top)
         picked = g_ref[...]
@@ -321,9 +321,17 @@
         for step in range(1, groups)
     ]
 
+    def near_first(step):
+        if outers != 4:
+            return lax.rem(outer + outers - step, outers)
+        low, high = lax.rem(outer, 2), outer // 2
+        flipped_low = 1 - low if step % 2 else low
+        flipped_high = 1 - high if step // 2 else high
+        return flipped_high * 2 + flipped_low
+
     def relay():
         for step in range(1, outers):
-            source = lax.rem(outer + outers - step, outers)
+            source = near_first(step)
             arrival, onward = came_p(source)
 
             def pass_on():
@@ -393,7 +401,7 @@
     x_ref[...] = x_all[...]
 
 
-def place_kernel(owners_ref, p_ref, x_ref, out_ref):
+def place_kernel(owners_ref, p_ref, x_ref, out_ref, probs_in, rows_in, placed, take, put):
     me = lax.axis_index("seq")
     fits = p_ref.shape[0]
     count = jnp.int32(0)
@@ -403,24 +411,36 @@
         for slot in range(SLOTS):
             chosen[slot] = jnp.where(mine & (count == slot), fit, chosen[slot])
         count = count + mine.astype(jnp.int32)
+    takes, puts = [], []
     for slot in range(SLOTS):
-
-        @pl.when(count > slot)
-        def _():
-            probs = p_ref[chosen[slot]]
-            rows = x_ref[chosen[slot]]
-            high = rows.astype(jnp.bfloat16)
-            low = (rows - high.astype(jnp.float32)).astype(jnp.bfloat16)
-            out_ref[0, slot] = lax.dot_general(
-                jnp.concatenate([probs, probs], axis=0),
-                jnp.concatenate([high, low], axis=0),
-                TN,
-                preferred_element_type=jnp.float32,
-            ).astype(jnp.bfloat16)
-
-        @pl.when(count <= slot)
-        def _():
-            out_ref[0, slot] = jnp.zeros(out_ref.shape[2:], jnp.bfloat16)
+        takes.append(
+            [
+                pltpu.make_async_copy(p_ref.at[chosen[slot]], probs_in.at[slot], take.at[0, slot]),
+                pltpu.make_async_copy(x_ref.at[chosen[slot]], rows_in.at[slot], take.at[1, slot]),
+            ]
+        )
+        for copy in takes[slot]:
+            copy.start()
+    for slot in range(SLOTS):
+        for copy in takes[slot]:
+            copy.wait()
+        probs = probs_in[slot]
+        rows = rows_in[slot]
+        high = rows.astype(jnp.bfloat16)
+        low = (rows - high.astype(jnp.float32)).astype(jnp.bfloat16)
+        fitted = lax.dot_general(
+            jnp.concatenate([probs, probs], axis=0),
+            jnp.concatenate([high, low], axis=0),
+            TN,
+            preferred_element_type=jnp.float32,
+        )
+        placed[slot] = jnp.where(count > slot, fitted, 0.0).astype(jnp.bfloat16)
+        puts.append(pltpu.make_async_copy(placed.at[slot], out_ref.at[0, slot], put.at[slot]))
+        if slot > 0:
+            puts[slot - 1].start()
+    puts[SLOTS - 1].start()
+    for copy in puts:
+        copy.wait()
 
 
 VMEM = pl.BlockSpec(memory_space=pltpu.VMEM)
@@ -498,8 +518,15 @@
     return pl.pallas_call(
         place_kernel,
         out_shape=jax.ShapeDtypeStruct((1, SLOTS, capacity, width), jnp.bfloat16),
-        in_specs=[SMEM, VMEM, VMEM],
-        out_specs=VMEM,
+        in_specs=[SMEM, ANY, ANY],
+        out_specs=ANY,
+        scratch_shapes=[
+            pltpu.VMEM((SLOTS, rows, capacity), jnp.bfloat16),
+            pltpu.VMEM((SLOTS, rows, width), jnp.float32),
+            pltpu.VMEM((SLOTS, capacity, width), jnp.bfloat16),
+            dma((2, SLOTS)),
+            dma((SLOTS,)),
+        ],
         compiler_params=pltpu.CompilerParams(**PARAMS),
     )(owners, probs, solved)
 

time: 46.9 us -> 47.1 us (level); the launches traced: 46.2 us -> 46.9 us
  Pallas kernels: 46.2 us -> 46.9 us
    pallas_call x1, Pallas kernels: 2.11 us -> 3.29 us  [on_device(): pl.pallas_call(place_kernel, out_shape=jax.ShapeDtypeStruct((1, SLOTS, ca...]
    pallas_call x1, Pallas kernels: 44.1 us -> 43.6 us  [on_device(): pl.pallas_call(fit_kernel, out_shape=(jax.ShapeDtypeStruct((fits, rows, c...]
where the time goes in v5:
time: 47.1 us; the launch traced here: 46.9 us
  Pallas kernels  46.9 us (100%)
    pallas_call x1, Pallas kernels, on_device(): pl.pallas_call(fit_kernel, out_shape=(jax.ShapeDtypeStruct((fits, rows, c...  43.6 us
    pallas_call x1, Pallas kernels, on_device(): pl.pallas_call(place_kernel, out_shape=jax.ShapeDtypeStruct((1, SLOTS, ca...  3.29 us

profile of v5, /device:TPU:0, one launch (start us, length us, event | category | flops | bytes accessed | tf_op | source)
XLA Modules:
  0.0 46.9 jit_solution(11764723050889282207)
XLA Ops:
  0.0 43.6 %shard_map.64 = (bf16[8,32,1024]{2,1,0:T(8,128)(2,1)}, f32[8,32,128]{2,1,0:T(8,128)}) custom-call(s32[1,8]{1,0:T(1,128)} %sizes_ref.1, bf16[8,128]{1,0:T(8,128)(2,1)} %bitcast.7, bf16[2,2048,128]{2,1,0:T(8,128)(2,1)} %bitcast.4, bf16[2,2048,128]{2,1,0:T(8,128)(2,1)} %bitcast.5, s32[8,1024]{1,0:T(8,128)} %bitcast.6), custom_call_target="tpu_custom_call" | custom-call | tf_op jit(solution)/shard_map/pallas_call | solution.py:462
  43.6 3.3 %shard_map.65 = bf16[1,3,1024,128]{3,2,1,0:T(8,128)(2,1)} custom-call(s32[1,8]{1,0:T(1,128)} %owners_ref.1, bf16[8,32,1024]{2,1,0:T(8,128)(2,1)} %get-tuple-element.7.p_ref, f32[8,32,128]{2,1,0:T(8,128)} %get-tuple-element.8.x_ref), custom_call_target="tpu_custom_call" | custom-call | tf_op jit(solution)/shard_map/pallas_call | solution.py:518
